TPU v7x, 32 devices: a whole 2x2x4 slice. The times are simulated.
32 devices in a mesh: section: 2 (over core), expert: 16 (over z, y, x).
Axes of the slice: x: 2, y: 2, z: 4, core: 2. Of those that a mesh axis runs over, the one named last changes fastest.
Arguments:
- act_in: bfloat16 [2, 2048, 7168], P('section', 'expert'), may hold values from -6 to 6
- cotangent: bfloat16 [2, 2048, 7168], P('section', 'expert'), may hold values from -6 to 6
- fwd_ids: int32 [2, 2048, 8], P('section', 'expert'), may hold values from 0 to 255, as said below
- fwd_gates: float32 [2, 2048, 8], P('section', 'expert'), may hold values from 0.05 to 0.8
- bwd_ids: int32 [2, 2048, 8], P('section', 'expert'), may hold values from 0 to 255, as said below
- bwd_gates: float32 [2, 2048, 8], P('section', 'expert'), may hold values from 0.05 to 0.8
- gate_w: bfloat16 [2, 7168, 2048], P('section', None, 'expert'), may hold values from -0.0625 to 0.0625
- up_w: bfloat16 [2, 7168, 2048], P('section', None, 'expert'), may hold values from -0.0625 to 0.0625
- down_w: bfloat16 [2, 2048, 7168], P('section', 'expert'), may hold values from -0.125 to 0.125
- gate_pre: bfloat16 [2, 160, 2048], P('section', None, 'expert'), may hold values from -6 to 6
- up_pre: bfloat16 [2, 160, 2048], P('section', None, 'expert'), may hold values from -6 to 6
Outputs:
- next_act: bfloat16 [2, 2048, 7168], P('section', 'expert')
- prev_grad: bfloat16 [2, 2048, 7168], P('section', 'expert')
- gate_grad: float32 [2, 2048, 8], P('section', 'expert')
Inputs may be any that keep to these rules, and one draw needn't show every extreme that they name: `fwd_ids`: the 8 ids of a row differ. In each aligned block of 128 rows (the rows of one device) each id below 1 is named by at most 10 rows; in every section one such id is named by exactly 10 rows in every block. `bwd_ids`: as for fwd_ids.
All inputs are finite; a program needn't handle non-finite values.
Results may differ from a plain program's by a relative error of at most 0.012.
Values may be sent and summed in bfloat16 or wider, within the bound.
A program may use at most 128 MiB of HBM per device.

v0:
```python
import functools
import math

import jax
import jax.numpy as jnp
import numpy as np
from jax import lax
from jax.experimental import pallas as pl
from jax.experimental.pallas import tpu as pltpu
from jax.sharding import PartitionSpec as P

FF = 2048
QUAD = 4
MESH = pl.DeviceIdType.MESH


def from_behind(value, axis, steps):
    count = lax.axis_size(axis)
    pairs = [(source, (source + steps) % count) for source in range(count)]
    return lax.ppermute(value, axis, pairs)


def routing(ids, gates, experts, capacity):
    expert_ids = jnp.arange(experts, dtype=jnp.int32)
    matches = ids[None, :, :] == expert_ids[:, None, None]
    routed = jnp.any(matches, axis=2)
    weights = jnp.sum(jnp.where(matches, gates[None, :, :], 0.0), axis=2)
    tokens = ids.shape[0]
    earlier = jnp.arange(tokens)[:, None] <= jnp.arange(tokens)[None, :]
    counted = jnp.sum(jnp.where(routed[:, :, None] & earlier[None], 1, 0), axis=1)
    position = counted - 1
    slot_ids = jnp.arange(capacity, dtype=jnp.int32)
    placing = (position[:, None, :] == slot_ids[None, :, None]) & routed[:, None, :]
    return (matches, placing.astype(jnp.float32), weights)


def xor(value, mask):
    out = value
    bit = 1
    while bit <= mask:
        if mask & bit:
            out = out + bit - 2 * bit * ((value // bit) % 2)
        bit *= 2
    return out


def dot(a, b, dims=((1,), (0,)), precision=None):
    return lax.dot_general(
        a, b, (dims, ((), ())), preferred_element_type=jnp.float32, precision=precision
    )


class Links:
    def __init__(self, send_sems, recv_sems):
        self.send_sems = send_sems
        self.recv_sems = recv_sems
        self.count = 0
        self.sent = []

    def copy(self, src, dst, peer, axis="expert"):
        k = self.count
        self.count += 1
        return pltpu.make_async_remote_copy(
            src_ref=src,
            dst_ref=dst,
            send_sem=self.send_sems.at[k],
            recv_sem=self.recv_sems.at[k],
            device_id={axis: peer},
            device_id_type=MESH,
        )

    def start(self, copy):
        copy.start()
        self.sent.append(copy)


def layer_kernel(
    slices,
    chunks,
    hop,
    tok_f,
    tok_b,
    w_gate,
    w_up,
    w_down,
    place_f,
    place_b,
    pre_gate,
    pre_up,
    rid_ref,
    fold_ref,
    unfold_ref,
    spread_ref,
    collect_ref,
    out_f,
    out_b,
    out_dots,
    tok,
    wc,
    wd,
    gat,
    par,
    rs1,
    rs2,
    rsz,
    hold,
    hold2,
    sums,
    landed,
    acc_ref,
    dot_ref,
    dot_got,
    local_sems,
    send_sems,
    recv_sems,
):
    device = lax.axis_index("expert")
    me = device % slices
    base = device - me
    lo = me % QUAD
    z = me // QUAD
    depth = slices // QUAD
    xp = base + xor(me, 1)
    yp = base + xor(me, 2)
    zp = [base + xor(z, q) * QUAD + lo for q in range(depth)]
    partners = [xp, yp] + zp[1:]
    width = wd.shape[2]
    ff = wd.shape[1]

    loads = []

    def load(src, dst):
        copy = pltpu.make_async_copy(src, dst, local_sems.at[len(loads)])
        loads.append(copy)
        copy.start()
        return copy

    load_tok = [load(tok_f, tok.at[0])]

    barrier = pltpu.get_barrier_semaphore()
    for peer in partners:
        pl.semaphore_signal(barrier, inc=1, device_id={"expert": peer}, device_id_type=MESH)
    greeted = len(partners)
    if hop:
        section = lax.axis_index("section")
        sections = lax.axis_size("section")
        ahead = (section + 1) % sections
        behind = (section + sections - 1) % sections
        for peer in (ahead, behind):
            pl.semaphore_signal(barrier, inc=1, device_id={"section": peer}, device_id_type=MESH)
        greeted += 2

    block_rows = gat.shape[2]
    group_rows = QUAD * block_rows
    places = (place_f, place_b)

    def place(mb):
        rid = rid_ref[:block_rows, :1]
        chosen = places[mb][...]
        total = jnp.zeros((block_rows, width), jnp.float32)
        for j in range(chunks):
            part = jnp.where(rid == j, chosen, 0.0).astype(jnp.bfloat16)
            total = total + dot(part, tok[mb, :, pl.ds(j * width, width)])
        gat[mb, me] = total.astype(jnp.bfloat16)

    links = Links(send_sems, recv_sems)

    def bid(q, mask):
        return xor(z, q) * QUAD + xor(lo, mask)

    order = list(range(1, depth)) + [0]
    steps = [(0, q) for q in range(depth)] + [(1, q) for q in order]
    tiles = width // 128
    cut = tiles // 2 * 128
    zsend, parts = {}, {}
    own_x, own_y, forward = {}, {}, {}
    r1, r2, rz = {}, {}, {}
    for step in steps:
        mb, q = step
        if step == steps[-1]:
            parts[step] = [(True, pl.ds(0, cut)), (False, pl.ds(cut, width - cut))]
        else:
            parts[step] = [(q % 2 == 0, pl.ds(0, width))]
        if q > 0:
            zsend[step] = links.copy(gat.at[mb, me], gat.at[mb, me], zp[q])
            rz[step] = links.copy(hold2.at[mb, q], rsz.at[mb, q], zp[q])
        own_x[step], own_y[step], forward[step], r1[step], r2[step] = [], [], [], [], []
        for first, cols in parts[step]:
            block = gat.at[mb, bid(q, 0), :, cols]
            own_x[step].append(links.copy(block, block, xp))
            own_y[step].append(links.copy(block, block, yp))
            got = gat.at[mb, bid(q, 2 if first else 1), :, cols]
            forward[step].append(links.copy(got, got, xp if first else yp))
            m1, p1, p2 = (1, xp, yp) if first else (2, yp, xp)
            r1[step].append([
                links.copy(par.at[mb, bid(q, 3), :, cols], rs1.at[mb, q, 1, :, cols], p1),
                links.copy(par.at[mb, bid(q, m1), :, cols], rs1.at[mb, q, 0, :, cols], p1),
            ])
            r2[step].append(links.copy(hold.at[mb, q, :, cols], rs2.at[mb, q, :, cols], p2))
    if hop:
        across = [
            links.copy(sums.at[0], landed.at[0], ahead, "section"),
            links.copy(sums.at[1], landed.at[1], behind, "section"),
        ]
    dx = links.copy(dot_ref.at[0], dot_got.at[0], xp)
    dy = links.copy(dot_ref.at[1], dot_got.at[1], yp)
    dz = [links.copy(dot_ref.at[2], dot_got.at[1 + q], zp[q]) for q in range(1, depth)]

    def own_sends(step):
        if step[1] > 0:
            zsend[step].wait_recv()
        for copy_x, copy_y in zip(own_x[step], own_y[step]):
            links.start(copy_x)
            links.start(copy_y)

    def start_mb(mb):
        for q in range(1, depth):
            links.start(zsend[mb, q])

    def do_forward(step):
        for k, (first, cols) in enumerate(parts[step]):
            (own_y if first else own_x)[step][k].wait_recv()
            links.start(forward[step][k])

    def compute(step):
        mb, q = step
        for k, (first, cols) in enumerate(parts[step]):
            (own_x if first else own_y)[step][k].wait_recv()
            forward[step][k].wait_recv()
        zq = xor(z, q)
        rid = rid_ref[...]
        group = pl.ds(zq * QUAD, QUAD)
        buf = gat[mb, group].reshape(group_rows, width)
        half = rid[:, :ff]
        fold = fold_ref[...]
        unfold = unfold_ref[...]
        if mb == 0:

            def gather_step(j, acc):
                return jnp.where(rid == j.astype(jnp.float32), dot(buf, wc[j]), acc)

            acc = lax.fori_loop(0, chunks, gather_step, jnp.zeros((group_rows, 2 * ff), jnp.float32))
            act = dot(fold, acc, precision=lax.Precision.HIGHEST)
            gate = act[:, :ff]
            hidden = gate / (1.0 + jnp.exp(-gate)) * act[:, ff:]
            spread = dot(unfold, hidden.astype(jnp.bfloat16))

            def piece(j, cols):
                part = jnp.where(half == j.astype(jnp.float32), spread, 0.0).astype(jnp.bfloat16)
                return dot(part, wd[j, :, cols])

        else:

            def gather_step(j, acc):
                return jnp.where(
                    half == j.astype(jnp.float32), dot(buf, wd[j], ((1,), (1,))), acc
                )

            acc = lax.fori_loop(0, chunks, gather_step, jnp.zeros((group_rows, ff), jnp.float32))
            grad = dot(fold, acc, precision=lax.Precision.HIGHEST)
            count = grad.shape[0]
            gate = pre_gate[zq].astype(jnp.float32)
            up = pre_up[zq].astype(jnp.float32)
            sig = 1.0 / (1.0 + jnp.exp(-gate))
            activated = gate * sig
            dots = jnp.sum(grad * activated * up, axis=1, keepdims=True)
            tile = dot(
                collect_ref[...], dots * spread_ref[...], precision=lax.Precision.HIGHEST
            )
            dot_ref[0, zq] = tile
            grad_gate = (grad * up * sig * (1.0 + gate * (1.0 - sig))).astype(jnp.bfloat16)
            grad_up = (grad * activated).astype(jnp.bfloat16)
            spread = jnp.concatenate([dot(unfold, grad_gate), dot(unfold, grad_up)], axis=1)

            def piece(j, cols):
                part = jnp.where(rid == j.astype(jnp.float32), spread, 0.0).astype(jnp.bfloat16)
                return dot(part, wc[j, cols, :], ((1,), (1,)))

        for k, (first, cols) in enumerate(parts[step]):
            acc_ref[:, cols] = piece(jnp.int32(0), cols)

            def out_step(j, carry):
                acc_ref[:, cols] += piece(j, cols)
                return carry

            lax.fori_loop(1, chunks, out_step, 0)
            done = acc_ref[:, cols].astype(jnp.bfloat16)
            par[mb, group, :, cols] = done.reshape(QUAD, block_rows, cols.size)
            for copy in r1[step][k]:
                links.start(copy)

    def wide(value):
        return value.astype(jnp.float32)

    def second(step):
        mb, q = step
        for k, (first, cols) in enumerate(parts[step]):
            r1[step][k][0].wait_recv()
            m2 = 2 if first else 1
            total = wide(par[mb, bid(q, m2), :, cols]) + wide(rs1[mb, q, 1, :, cols])
            hold[mb, q, :, cols] = total.astype(jnp.bfloat16)
            links.start(r2[step][k])

    def third(step):
        mb, q = step
        for k, (first, cols) in enumerate(parts[step]):
            r1[step][k][1].wait_recv()
            r2[step][k].wait_recv()
            total = wide(par[mb, bid(q, 0), :, cols]) + wide(rs1[mb, q, 0, :, cols])
            total = total + wide(rs2[mb, q, :, cols])
            hold2[mb, q, :, cols] = total.astype(jnp.bfloat16)
        if q > 0:
            links.start(rz[step])

    def finish(mb):
        total = wide(hold2[mb, 0])
        for q in range(1, depth):
            rz[mb, q].wait_recv()
            total = total + wide(rsz[mb, q])
        sums[mb] = total.astype(jnp.bfloat16)
        if hop:
            links.start(across[mb])

    def deliver(mb, out):
        if hop:
            across[mb].wait_recv()
            out[...] = landed[mb]
        else:
            out[...] = sums[mb]

    load_tok[0].wait()
    load_tok.append(load(tok_b, tok.at[1]))
    load_w = []
    for j in range(chunks):
        rows = pl.ds(j * width, width)
        load_w.append(load(w_gate.at[rows, :], wc.at[j, :, pl.ds(0, ff)]))
        load_w.append(load(w_up.at[rows, :], wc.at[j, :, pl.ds(ff, ff)]))
        load_w.append(load(w_down.at[:, rows], wd.at[j]))
    place(0)
    pl.semaphore_wait(barrier, greeted)
    own_sends(steps[0])
    start_mb(0)
    load_tok[1].wait()
    place(1)
    start_mb(1)
    count = len(steps)
    for t in range(count + 3):
        if t + 1 < count:
            own_sends(steps[t + 1])
        if t < count:
            do_forward(steps[t])
        if t == 0:
            for copy in load_w:
                copy.wait()
        if 0 <= t - 1 < count:
            compute(steps[t - 1])
        if t - 1 == count - 1:
            links.start(dx)
        if 0 <= t - 2 < count:
            second(steps[t - 2])
        if t - 2 == count - 1:
            dx.wait_recv()
            dot_ref[1] = dot_ref[0] + dot_got[0]
            links.start(dy)
        if 0 <= t - 3 < count:
            third(steps[t - 3])
        if t == count:
            finish(0)
        if t == count + 1:
            deliver(0, out_f)
    dy.wait_recv()
    dot_ref[2] = dot_ref[1] + dot_got[1]
    for copy in dz:
        links.start(copy)
    finish(1)
    total = dot_ref[2]
    for q in range(1, depth):
        dz[q - 1].wait_recv()
        total = total + dot_got[1 + q]
    out_dots[...] = total
    deliver(1, out_b)
    for copy in links.sent:
        copy.wait_send()


def run_layer(tok_f, tok_b, w_gate, w_up, w_down, place_f, place_b, pre_gate, pre_up, slices, rows, hop):
    features = tok_f.shape[1]
    chunks = 16 // math.gcd(16, rows)
    width = features // chunks
    ff = w_gate.shape[1]
    depth = slices // QUAD
    block_rows = chunks * rows
    group_rows = QUAD * block_rows
    group_slots = QUAD * rows

    row = np.arange(group_rows)
    slot = (row // block_rows) * rows + row % rows
    rid = np.broadcast_to((row % block_rows // rows)[:, None], (group_rows, 2 * ff))
    rid = rid.astype(np.float32)
    unfold = slot[:, None] == np.arange(group_slots)[None, :]
    fold = unfold.T.astype(np.float32)
    unfold = unfold.astype(jnp.bfloat16)
    slots = np.arange(group_slots)
    spread = (slots[:, None] % rows == np.arange(128)[None, :]).astype(np.float32)
    collect = (slots[None, :] // rows == np.arange(8)[:, None]).astype(np.float32)

    vmem = pl.BlockSpec(memory_space=pltpu.VMEM)
    anywhere = pl.BlockSpec(memory_space=pl.ANY)
    block = (block_rows, width)
    sems = 2 * (depth * 6 + 2 * (depth - 1)) + 6 + 2 + depth - 1 + 2
    return pl.pallas_call(
        functools.partial(layer_kernel, slices, chunks, hop),
        out_shape=(
            jax.ShapeDtypeStruct(block, jnp.bfloat16),
            jax.ShapeDtypeStruct(block, jnp.bfloat16),
            jax.ShapeDtypeStruct((depth, 8, 128), jnp.float32),
        ),
        in_specs=[anywhere] * 5 + [vmem] * 9,
        out_specs=(vmem, vmem, vmem),
        scratch_shapes=[
            pltpu.VMEM((2,) + tok_f.shape, jnp.bfloat16),
            pltpu.VMEM((chunks, width, 2 * ff), jnp.bfloat16),
            pltpu.VMEM((chunks, ff, width), jnp.bfloat16),
            pltpu.VMEM((2, slices) + block, jnp.bfloat16),
            pltpu.VMEM((2, slices) + block, jnp.bfloat16),
            pltpu.VMEM((2, depth, 2) + block, jnp.bfloat16),
            pltpu.VMEM((2, depth) + block, jnp.bfloat16),
            pltpu.VMEM((2, depth) + block, jnp.bfloat16),
            pltpu.VMEM((2, depth) + block, jnp.bfloat16),
            pltpu.VMEM((2, depth) + block, jnp.bfloat16),
            pltpu.VMEM((2,) + block, jnp.bfloat16),
            pltpu.VMEM((2,) + block, jnp.bfloat16),
            pltpu.VMEM((group_rows, width), jnp.float32),
            pltpu.VMEM((3, depth, 8, 128), jnp.float32),
            pltpu.VMEM((1 + depth, depth, 8, 128), jnp.float32),
            pltpu.SemaphoreType.DMA((2 + 3 * chunks,)),
            pltpu.SemaphoreType.DMA((sems,)),
            pltpu.SemaphoreType.DMA((sems,)),
        ],
        compiler_params=pltpu.CompilerParams(
            collective_id=0, has_side_effects=True, vmem_limit_bytes=56 * 2**20
        ),
        name="moe_layer",
    )(tok_f, tok_b, w_gate, w_up, w_down, place_f, place_b, pre_gate, pre_up,
      rid, fold, unfold, spread, collect)


def mix_kernel(rows, block_f, block_b, weight_f, weight_b, out_f, out_b):
    block_rows, width = block_f.shape
    j = pl.program_id(0)
    low = j * rows
    column = lax.broadcasted_iota(jnp.int32, weight_f.shape, 1)
    upper = column >= block_rows
    place = jnp.where(upper, column - block_rows, column)
    inside = (place >= low) & (place < low + rows)
    for block, weight, out in ((block_f, weight_f, out_f), (block_b, weight_b, out_b)):
        wanted = jnp.where(inside, weight[...], 0.0)
        high = wanted.astype(jnp.bfloat16).astype(jnp.float32)
        both = jnp.where(upper, wanted - high, high).astype(jnp.bfloat16)
        table = jnp.concatenate([block[...], block[...]], axis=0)
        out[...] = dot(both, table).astype(jnp.bfloat16)


def mix(block_f, block_b, weight_f, weight_b, rows):
    block_rows, width = block_f.shape
    tokens = weight_f.shape[0]
    chunks = block_rows // rows
    whole = pl.BlockSpec(block_f.shape, lambda j: (0, 0))
    weights = pl.BlockSpec(weight_f.shape, lambda j: (0, 0))
    piece = pl.BlockSpec((tokens, width), lambda j: (0, j))
    shape = jax.ShapeDtypeStruct((tokens, chunks * width), jnp.bfloat16)
    return pl.pallas_call(
        functools.partial(mix_kernel, rows),
        out_shape=(shape, shape),
        grid=(chunks,),
        in_specs=[whole, whole, weights, weights],
        out_specs=(piece, piece),
        name="mix",
    )(block_f, block_b, weight_f, weight_b)


def body(
    act_in,
    cotangent,
    fwd_ids,
    fwd_gates,
    bwd_ids,
    bwd_gates,
    gate_w,
    up_w,
    down_w,
    gate_pre,
    up_pre,
):
    ndev = lax.axis_size("expert")
    ff_dev = gate_w.shape[2]
    slices = FF // ff_dev
    experts = ndev // slices
    capacity = gate_pre.shape[1] // ndev
    rows = experts * capacity
    chunks = 16 // math.gcd(16, rows)
    features = act_in.shape[2]
    width = features // chunks
    depth = slices // QUAD
    columns = [[g * slices + i for g in range(experts)] for i in range(slices)]

    def exchange(value):
        return lax.all_to_all(
            value, "expert", split_axis=0, concat_axis=0, axis_index_groups=columns, tiled=True
        )

    matches_f, placing_f, weights_f = routing(fwd_ids[0], fwd_gates[0], experts, capacity)
    matches_b, placing_b, weights_b = routing(bwd_ids[0], bwd_gates[0], experts, capacity)

    def prepare(tokens, placing):
        chosen = placing.reshape(rows, tokens.shape[0])
        if experts > 1:
            picked = dot(chosen.astype(jnp.bfloat16), tokens).astype(jnp.bfloat16)
            picked = exchange(picked.reshape(experts, capacity, features))
            tokens = picked.reshape(rows, features)
            chosen = jnp.eye(rows, dtype=jnp.float32)
        return tokens, jnp.tile(chosen, (chunks, 1))

    tok_f, place_f = prepare(act_in[0], placing_f)
    tok_b, place_b = prepare(cotangent[0], placing_b)

    def by_group(saved):
        saved = saved.reshape(experts, slices, capacity, ff_dev).transpose(1, 0, 2, 3)
        return saved.reshape(depth, QUAD * rows, ff_dev)

    block_f, block_b, dots = run_layer(
        tok_f, tok_b, gate_w[0], up_w[0], down_w[0], place_f, place_b,
        by_group(gate_pre[0]), by_group(up_pre[0]), slices, rows, experts == 1,
    )
    me = lax.axis_index("expert") % slices
    mine = lax.dynamic_slice(dots, (me // QUAD, me % QUAD, 0), (1, 1, 128))
    mine = mine[0, 0, :rows].reshape(experts, capacity)

    def send_back(block):
        table = block.reshape(chunks, rows, width).transpose(1, 0, 2)
        table = exchange(table.reshape(experts, capacity, features))
        table = table.reshape(rows, chunks, width).transpose(1, 0, 2)
        return table.reshape(chunks * rows, width)

    if experts > 1:
        block_f = send_back(block_f)
        block_b = send_back(block_b)
        mine = exchange(mine)

    token_dots = jnp.sum(placing_b * mine[:, :, None], axis=1)
    gate_grad = jnp.sum(jnp.where(matches_b, token_dots[:, :, None], 0.0), axis=0)

    def weight_table(placing, weights):
        table = (placing * weights[:, None, :]).reshape(rows, -1).T
        return jnp.tile(table, (1, 2 * chunks))

    weight_f = from_behind(weight_table(placing_f, weights_f), "section", 1)
    weight_b = from_behind(weight_table(placing_b, weights_b), "section", -1)
    if experts > 1:
        block_f = from_behind(block_f, "section", 1)
        block_b = from_behind(block_b, "section", -1)
    next_act, prev_grad = mix(block_f, block_b, weight_f, weight_b, rows)
    return (next_act[None], prev_grad[None], gate_grad[None])


def solution(mesh):
    in_specs = (
        P("section", "expert", None),
        P("section", "expert", None),
        P("section", "expert", None),
        P("section", "expert", None),
        P("section", "expert", None),
        P("section", "expert", None),
        P("section", None, "expert"),
        P("section", None, "expert"),
        P("section", "expert", None),
        P("section", None, "expert"),
        P("section", None, "expert"),
    )
    out_specs = (
        P("section", "expert", None),
        P("section", "expert", None),
        P("section", "expert", None),
    )
    return jax.shard_map(body, mesh=mesh, in_specs=in_specs, out_specs=out_specs, check_vma=False)
```

profile of v0, /device:TPU:1, one launch (start us, length us, event | category | flops | bytes accessed | tf_op | source)
XLA Modules:
  0.0 120.7 jit_solution(7504975448599104932)
XLA Ops:
  0.6 0.7 select_reduce_fusion.2
  1.4 0.1 select_reduce_fusion
  1.5 0.1 copy.22
  1.6 0.1 collective-permute-start.1
  1.7 0.7 select_reduce_fusion.3
  2.5 0.1 select_reduce_fusion.1
  2.6 0.1 copy.21
  2.7 0.6 collective-permute-start
  3.3 0.6 tile.37.place_b
  4.0 0.6 tile.17.place_f
  4.6 108.6 %moe_layer.1 = (bf16[80,896]{1,0:T(8,128)(2,1)}, bf16[80,896]{1,0:T(8,128)(2,1)}, f32[4,8,128]{2,1,0:T(8,128)}) custom-call(bf16[128,7168]{1,0:T(8,128)(2,1)} %bitcast.15, bf16[128,7168]{1,0:T(8,128)(2,1)} %bitcast.16, bf16[7168,128]{1,0:T(8,128)(2,1)} %bitcast.17, bf16[7168,128]{1,0:T(8,128)(2,1)} %bitcast.18, bf16[128,7168]{1,0:T(8,128)(2,1)} %bitcast.19, ...), custom_call_target="tpu_custom_call" | custom-call | tf_op jit(solution)/shard_map/moe_layer/pallas_call | solution.py:411
  113.2 0.7 constant_dynamic-slice_fusion
  113.9 0.1 fusion.10
  114.0 0.6 broadcast_select_fusion
  114.6 0.0 collective-permute-done.1.weight_b
  114.6 0.0 copy-start
  114.6 0.0 collective-permute-done.weight_f
  114.6 0.0 copy-start.1
  114.6 0.6 copy-done
  115.3 0.1 copy-done.1
  115.3 5.4 %mix.1 = (bf16[128,7168]{1,0:T(8,128)(2,1)}, bf16[128,7168]{1,0:T(8,128)(2,1)}) custom-call(bf16[80,896]{1,0:T(8,128)(2,1)} %get-tuple-element.8.block_f, bf16[80,896]{1,0:T(8,128)(2,1)} %get-tuple-element.9.block_b, f32[128,160]{1,0:T(8,128)} %copy-done.1, f32[128,160]{1,0:T(8,128)} %copy-done), custom_call_target="tpu_custom_call" | custom-call | tf_op jit(solution)/shard_map/mix/pallas_call | solution.py:472
  (15 shorter events, 0.1 us)
Async XLA Ops:
  1.6 113.0 %collective-permute-start.1 = (f32[128,160]{1,0:T(8,128)S(1)}, f32[128,160]{1,0:T(8,128)S(1)}, u32[]{:S(2)}, u32[]{:S(2)}) collective-permute-start(f32[128,160]{1,0:T(8,128)S(1)} %copy.22), channel_id=1, source_target_pairs={{0,16},{16,0},{1,17},{17,1},{2,18},{18,2},{3,19},{19,3},{4,20},{20... | collective-permute-start | bytes 245768 | tf_op jit(solution)/shard_map/ppermute | solution.py:20
  2.7 111.9 %collective-permute-start = (f32[128,160]{1,0:T(8,128)S(1)}, f32[128,160]{1,0:T(8,128)S(1)}, u32[]{:S(2)}, u32[]{:S(2)}) collective-permute-start(f32[128,160]{1,0:T(8,128)S(1)} %copy.21), channel_id=1, source_target_pairs={{0,16},{16,0},{1,17},{17,1},{2,18},{18,2},{3,19},{19,3},{4,20},{20... | collective-permute-start | bytes 245768 | tf_op jit(solution)/shard_map/ppermute | solution.py:20
  114.6 0.6 copy-start
  114.6 0.7 copy-start.1
where the time goes:
time: 121 us
  Pallas kernels  114 us (94%)
  local copies, waits for them, and re-layouts  2.87 us (2%)
  other arithmetic  2.42 us (2%)
    pallas_call x1, Pallas kernels, run_layer(): pl.pallas_call(functools.partial(layer_kernel, slices, chunks, hop), out_...  109 us
    pallas_call x1, Pallas kernels, mix(): pl.pallas_call(functools.partial(mix_kernel, rows), out_shape=(shape, sha...  5.36 us
  transfers between devices with their start and end apart: 2, of which 0 were waited for; matrix products, arithmetic and copies ran while one was open for 3% of the time, Pallas kernels for 90%

commit v1 on v0

v1 whole, which is shorter than its diff:
```python
import functools
import math

import jax
import jax.numpy as jnp
from jax import lax
from jax.experimental import pallas as pl
from jax.experimental.pallas import tpu as pltpu
from jax.sharding import PartitionSpec as P

FF = 2048
QUAD = 4
LANES = 128
AHEAD = 3
SECOND_LAG = 1
THIRD_LAG = 2
SEMAPHORES = 128
MESH = pl.DeviceIdType.MESH


def from_behind(value, axis, steps):
    count = lax.axis_size(axis)
    pairs = [(source, (source + steps) % count) for source in range(count)]
    return lax.ppermute(value, axis, pairs)


def routing(ids, gates, experts, capacity):
    expert_ids = jnp.arange(experts, dtype=jnp.int32)
    matches = ids[None, :, :] == expert_ids[:, None, None]
    routed = jnp.any(matches, axis=2)
    weights = jnp.sum(jnp.where(matches, gates[None, :, :], 0.0), axis=2)
    tokens = ids.shape[0]
    earlier = jnp.arange(tokens)[:, None] <= jnp.arange(tokens)[None, :]
    counted = jnp.sum(jnp.where(routed[:, :, None] & earlier[None], 1, 0), axis=1)
    position = counted - 1
    slot_ids = jnp.arange(capacity, dtype=jnp.int32)
    placing = (position[:, None, :] == slot_ids[None, :, None]) & routed[:, None, :]
    return (matches, placing.astype(jnp.float32), weights)


def xor(value, mask):
    out = value
    bit = 1
    while bit <= mask:
        if mask & bit:
            out = out + bit - 2 * bit * ((value // bit) % 2)
        bit *= 2
    return out


def dot(a, b, dims=((1,), (0,))):
    return lax.dot_general(a, b, (dims, ((), ())), preferred_element_type=jnp.float32)


def wide(value):
    return value.astype(jnp.float32)


def narrow(value):
    return value.astype(jnp.bfloat16)


def padded(rows):
    return -(-rows // 16) * 16


def selection(count, rows, pad, flip=False):
    shape = (count * rows, count * pad) if flip else (count * pad, count * rows)
    long = lax.broadcasted_iota(jnp.int32, shape, 1 if flip else 0)
    short = lax.broadcasted_iota(jnp.int32, shape, 0 if flip else 1)
    piece = lax.shift_right_logical(long, jnp.int32(pad.bit_length() - 1))
    inner = long & (pad - 1)
    chosen = (short == piece * rows + inner) & (inner < rows)
    return narrow(jnp.where(chosen, 1.0, 0.0))


def slot_table(ids, rows):
    tokens = ids.shape[0]
    hit = jnp.where(ids == 0, 1.0, 0.0)
    routed = jnp.max(hit, axis=1, keepdims=True)
    spread = jnp.broadcast_to(routed, (tokens, LANES))
    row = lax.broadcasted_iota(jnp.int32, (tokens, tokens), 0)
    column = lax.broadcasted_iota(jnp.int32, (tokens, tokens), 1)
    lower = narrow(jnp.where(column <= row, 1.0, 0.0))
    rank = dot(lower, narrow(spread)) - 1.0
    lane = wide(lax.broadcasted_iota(jnp.int32, (tokens, LANES), 1))
    return jnp.where((rank == lane) & (spread > 0.0), 1.0, 0.0)


class Links:
    def __init__(self, send_sems, recv_sems):
        self.send_sems = send_sems
        self.recv_sems = recv_sems
        self.count = 0
        self.sent = []

    def copy(self, src, dst, peer, axis="expert"):
        k = self.count
        self.count += 1
        assert k < SEMAPHORES
        return pltpu.make_async_remote_copy(
            src_ref=src,
            dst_ref=dst,
            send_sem=self.send_sems.at[k],
            recv_sem=self.recv_sems.at[k],
            device_id={axis: peer},
            device_id_type=MESH,
        )

    def start(self, copy):
        copy.start()
        self.sent.append(copy)


def layer_kernel(slices, chunks, rows, hop, *refs):
    inputs = 11 if hop else 7
    tok_f, tok_b, w_gate, w_up, w_down, pre_gate, pre_up = refs[:7]
    routes = refs[7:inputs]
    outs = 4 if hop else 3
    out_f, out_b, out_dots = refs[inputs : inputs + 3]
    (
        tok, wc, wd, gat, par, xb, yb, pre, rs1, rs2, rsz, hold, hold2, sums, landed, table,
        table_got, dot_out, dot_in, local_sems, send_sems, recv_sems,
    ) = refs[inputs + outs :]
    device = lax.axis_index("expert")
    me = device % slices
    base = device - me
    lo = me % QUAD
    z = me // QUAD
    depth = slices // QUAD
    xp = base + xor(me, 1)
    yp = base + xor(me, 2)
    zp = [base + xor(z, q) * QUAD + lo for q in range(depth)]
    features, ff = wc.shape[0], wd.shape[0]
    width = features // chunks
    pad = padded(rows)

    def bid(q, mask):
        return xor(z, q) * QUAD + xor(lo, mask)

    def cols_of(j):
        return pl.ds(j * width, width)

    loads = []

    def load(src, dst):
        copy = pltpu.make_async_copy(src, dst, local_sems.at[len(loads)])
        loads.append(copy)
        copy.start()
        return copy

    load_f = [load(tok_f.at[:, cols_of(j)], tok.at[0, :, cols_of(j)]) for j in range(chunks)]

    barrier = pltpu.get_barrier_semaphore()
    peers = [(q, m) for q in range(depth) for m in range(QUAD) if q or m]
    for q, m in peers:
        pl.semaphore_signal(
            barrier, inc=1, device_id={"expert": base + bid(q, m)}, device_id_type=MESH
        )
    greeted = len(peers)
    if hop:
        section = lax.axis_index("section")
        sections = lax.axis_size("section")
        ahead = (section + 1) % sections
        behind = (section + sections - 1) % sections
        for peer in (ahead, behind):
            pl.semaphore_signal(barrier, inc=1, device_id={"section": peer}, device_id_type=MESH)
        greeted += 2

    load_b = [load(tok_b.at[:, cols_of(j)], tok.at[1, :, cols_of(j)]) for j in range(chunks)]
    load_w = []
    for j in range(chunks):
        load_w.append(load(w_gate.at[cols_of(j), :], wc.at[cols_of(j), pl.ds(0, ff)]))
        load_w.append(load(w_up.at[cols_of(j), :], wc.at[cols_of(j), pl.ds(ff, ff)]))
        load_w.append(load(w_down.at[:, cols_of(j)], wd.at[:, cols_of(j)]))

    unpack = selection(chunks, rows, pad)
    pack = selection(chunks, rows, pad, flip=True)

    def choose(mb):
        if not hop:
            shape = (pad, tok.shape[1])
            same = lax.broadcasted_iota(jnp.int32, shape, 0)
            return narrow(
                jnp.where(same == lax.broadcasted_iota(jnp.int32, shape, 1), 1.0, 0.0)
            )
        ids = routes[2 * mb][...]
        slots = slot_table(ids, rows)
        gates = jnp.where(ids == 0, routes[2 * mb + 1][...], 0.0)
        table[mb] = slots * jnp.sum(gates, axis=1, keepdims=True)
        return narrow(jnp.transpose(slots)[:pad])

    def place(mb, chosen, waits):
        for j in range(chunks):
            waits[j].wait()
            picked = dot(chosen, tok[mb, :, cols_of(j)])
            yb[0, pl.ds(j * pad, pad), :] = narrow(picked)
        gat[mb, me] = narrow(dot(pack, yb[0]))

    links = Links(send_sems, recv_sems)

    order = list(range(1, depth)) + [0]
    steps = [(0, q) for q in range(depth)] + [(1, q) for q in order]
    tiles = width // LANES
    cut = tiles // 2 * LANES
    zsend, parts = {}, {}
    own_x, own_y, forward = {}, {}, {}
    r1, r2, rz, dots_sent = {}, {}, {}, {}
    for step in steps:
        mb, q = step
        if step == steps[-1]:
            parts[step] = [(True, pl.ds(0, cut)), (False, pl.ds(cut, width - cut))]
        else:
            parts[step] = [(q % 2 == 0, pl.ds(0, width))]
        if q > 0:
            zsend[step] = links.copy(gat.at[mb, me], gat.at[mb, me], zp[q])
            rz[step] = links.copy(hold2.at[mb, q], rsz.at[mb, q], zp[q])
        own_x[step], own_y[step], forward[step], r1[step], r2[step] = [], [], [], [], []
        for first, cols in parts[step]:
            block = gat.at[mb, bid(q, 0), :, cols]
            own_x[step].append(links.copy(block, block, xp))
            own_y[step].append(links.copy(block, block, yp))
            got = gat.at[mb, bid(q, 2 if first else 1), :, cols]
            forward[step].append(links.copy(got, got, xp if first else yp))
            m1, p1, p2 = (1, xp, yp) if first else (2, yp, xp)
            r1[step].append([
                links.copy(par.at[mb, bid(q, 3), :, cols], rs1.at[mb, q, 1, :, cols], p1),
                links.copy(par.at[mb, bid(q, m1), :, cols], rs1.at[mb, q, 0, :, cols], p1),
            ])
            r2[step].append(links.copy(hold.at[mb, q, :, cols], rs2.at[mb, q, :, cols], p2))
        if mb == 1:
            dots_sent[q] = [
                links.copy(dot_out.at[bid(q, m)], dot_in.at[q * QUAD + m], base + bid(q, m))
                for m in range(QUAD)
                if q or m
            ]
    if hop:
        across = [
            links.copy(sums.at[0], landed.at[0], ahead, "section"),
            links.copy(sums.at[1], landed.at[1], behind, "section"),
        ]
        tables = [
            links.copy(table.at[0], table_got.at[0], ahead, "section"),
            links.copy(table.at[1], table_got.at[1], behind, "section"),
        ]

    def do_own(step):
        if step[1] > 0:
            zsend[step].wait_recv()
        for copy_x, copy_y in zip(own_x[step], own_y[step]):
            links.start(copy_x)
            links.start(copy_y)

    def start_mb(mb):
        for q in range(1, depth):
            links.start(zsend[mb, q])

    def do_forward(step):
        for k, (first, cols) in enumerate(parts[step]):
            (own_y if first else own_x)[step][k].wait_recv()
            links.start(forward[step][k])

    def compute(step):
        mb, q = step
        for k, (first, cols) in enumerate(parts[step]):
            (own_x if first else own_y)[step][k].wait_recv()
            forward[step][k].wait_recv()
        zq = xor(z, q)
        group = zq * QUAD
        for b in range(QUAD):
            full = narrow(dot(unpack, gat[mb, group + b]))
            for j in range(chunks):
                xb[pl.ds(b * pad, pad), cols_of(j)] = full[j * pad : (j + 1) * pad]
        total = None
        for j in range(chunks):
            if mb == 0:
                part = dot(xb[:, cols_of(j)], wc[cols_of(j), :])
            else:
                part = dot(xb[:, cols_of(j)], wd[:, cols_of(j)], ((1,), (1,)))
            total = part if total is None else total + part
        if mb == 0:
            gate = total[:, :ff]
            hidden = narrow(gate / (1.0 + jnp.exp(-gate)) * total[:, ff:])

            def piece(j):
                return dot(hidden, wd[:, cols_of(j)])

        else:
            gate = wide(pre[0, zq])
            up = wide(pre[1, zq])
            sig = 1.0 / (1.0 + jnp.exp(-gate))
            activated = gate * sig
            dots = jnp.sum(total * activated * up, axis=1, keepdims=True)
            shape = (QUAD * pad, LANES)
            inner = lax.broadcasted_iota(jnp.int32, shape, 0) & (pad - 1)
            lane = lax.broadcasted_iota(jnp.int32, shape, 1)
            placed = jnp.where(inner == lane, dots, 0.0)
            for b in range(QUAD):
                line = jnp.sum(placed[b * pad : (b + 1) * pad], axis=0, keepdims=True)
                dot_out[group + b] = jnp.broadcast_to(line, (8, LANES))
            for copy in dots_sent[q]:
                links.start(copy)
            grad_gate = narrow(total * up * sig * (1.0 + gate * (1.0 - sig)))
            both = jnp.concatenate([grad_gate, narrow(total * activated)], axis=1)

            def piece(j):
                return dot(both, wc[cols_of(j), :], ((1,), (1,)))

        for j in range(chunks):
            full = narrow(piece(j))
            for b in range(QUAD):
                yb[b, pl.ds(j * pad, pad), :] = full[b * pad : (b + 1) * pad]
        for b in range(QUAD):
            par[mb, group + b] = narrow(dot(pack, yb[b]))
        for copies in r1[step]:
            for copy in copies:
                links.start(copy)

    def second(step):
        mb, q = step
        for k, (first, cols) in enumerate(parts[step]):
            r1[step][k][0].wait_recv()
            m2 = 2 if first else 1
            total = wide(par[mb, bid(q, m2), :, cols]) + wide(rs1[mb, q, 1, :, cols])
            hold[mb, q, :, cols] = narrow(total)
            links.start(r2[step][k])

    def third(step):
        mb, q = step
        for k, (first, cols) in enumerate(parts[step]):
            r1[step][k][1].wait_recv()
            r2[step][k].wait_recv()
            total = wide(par[mb, bid(q, 0), :, cols]) + wide(rs1[mb, q, 0, :, cols])
            total = total + wide(rs2[mb, q, :, cols])
            hold2[mb, q, :, cols] = narrow(total)
        if q > 0:
            links.start(rz[step])

    def finish(mb):
        total = wide(hold2[mb, 0])
        for q in range(1, depth):
            rz[mb, q].wait_recv()
            total = total + wide(rsz[mb, q])
        sums[mb] = narrow(total)
        if hop:
            links.start(across[mb])

    def deliver(mb, out):
        if hop:
            across[mb].wait_recv()
            out[...] = landed[mb]
        else:
            out[...] = sums[mb]

    place(0, choose(0), load_f)
    pl.semaphore_wait(barrier, greeted)
    do_own(steps[0])
    start_mb(0)
    place(1, choose(1), load_b)
    start_mb(1)
    if hop:
        for copy in tables:
            links.start(copy)
    spaced = selection(slices, rows, pad)
    for k, saved in enumerate((pre_gate, pre_up)):
        pre[k] = narrow(dot(spaced, saved[...])).reshape(pre.shape[1:])

    count = len(steps)
    gathers = [(do_own, s) for s in range(1)]
    for s in range(1, count):
        gathers += [(do_own, s), (do_forward, s - 1)]
    gathers = gathers[1:] + [(do_forward, count - 1)]

    def gather_to(s):
        while gathers and (do_forward, min(s, count - 1)) in gathers:
            event, at = gathers.pop(0)
            event(steps[at])

    for t in range(count + THIRD_LAG):
        gather_to(t + AHEAD - 1)
        if t == 0:
            for copy in load_w:
                copy.wait()
        if t < count:
            compute(steps[t])
        if 0 <= t - SECOND_LAG < count:
            second(steps[t - SECOND_LAG])
        if 0 <= t - THIRD_LAG < count:
            third(steps[t - THIRD_LAG])
        if t == count - 1:
            finish(0)
        if t == count:
            deliver(0, out_f)
    total = dot_out[me]
    for q in range(depth):
        for copy in dots_sent[q]:
            copy.wait_recv()
    for q, m in peers:
        total = total + dot_in[q * QUAD + m]
    out_dots[...] = total
    if hop:
        out_tables = refs[inputs + 3]
        for k in range(2):
            tables[k].wait_recv()
            out_tables[k] = table_got[k]
    finish(1)
    deliver(1, out_b)
    for copy in links.sent:
        copy.wait_send()


def run_layer(tok_f, tok_b, w_gate, w_up, w_down, pre_gate, pre_up, routes, slices, rows):
    hop = bool(routes)
    features = tok_f.shape[1]
    chunks = 16 // math.gcd(16, rows)
    width = features // chunks
    ff = w_gate.shape[1]
    depth = slices // QUAD
    pad = padded(rows)
    group = QUAD * pad

    vmem = pl.BlockSpec(memory_space=pltpu.VMEM)
    anywhere = pl.BlockSpec(memory_space=pl.ANY)
    block = (chunks * rows, width)
    tables = (2, tok_f.shape[0] if hop else 8, LANES)
    out_shape = [
        jax.ShapeDtypeStruct(block, jnp.bfloat16),
        jax.ShapeDtypeStruct(block, jnp.bfloat16),
        jax.ShapeDtypeStruct((8, LANES), jnp.float32),
    ]
    if hop:
        out_shape.append(jax.ShapeDtypeStruct(tables, jnp.float32))
    return pl.pallas_call(
        functools.partial(layer_kernel, slices, chunks, rows, hop),
        out_shape=tuple(out_shape),
        in_specs=[anywhere] * 5 + [vmem] * (2 + len(routes)),
        out_specs=(vmem,) * len(out_shape),
        scratch_shapes=[
            pltpu.VMEM((2,) + tok_f.shape, jnp.bfloat16),
            pltpu.VMEM((features, 2 * ff), jnp.bfloat16),
            pltpu.VMEM((ff, features), jnp.bfloat16),
            pltpu.VMEM((2, slices) + block, jnp.bfloat16),
            pltpu.VMEM((2, slices) + block, jnp.bfloat16),
            pltpu.VMEM((group, features), jnp.bfloat16),
            pltpu.VMEM((QUAD, chunks * pad, width), jnp.bfloat16),
            pltpu.VMEM((2, depth, group, ff), jnp.bfloat16),
            pltpu.VMEM((2, depth, 2) + block, jnp.bfloat16),
            pltpu.VMEM((2, depth) + block, jnp.bfloat16),
            pltpu.VMEM((2, depth) + block, jnp.bfloat16),
            pltpu.VMEM((2, depth) + block, jnp.bfloat16),
            pltpu.VMEM((2, depth) + block, jnp.bfloat16),
            pltpu.VMEM((2,) + block, jnp.bfloat16),
            pltpu.VMEM((2,) + block, jnp.bfloat16),
            pltpu.VMEM(tables, jnp.float32),
            pltpu.VMEM(tables, jnp.float32),
            pltpu.VMEM((slices, 8, LANES), jnp.float32),
            pltpu.VMEM((slices, 8, LANES), jnp.float32),
            pltpu.SemaphoreType.DMA((5 * chunks,)),
            pltpu.SemaphoreType.DMA((SEMAPHORES,)),
            pltpu.SemaphoreType.DMA((SEMAPHORES,)),
        ],
        compiler_params=pltpu.CompilerParams(
            collective_id=0, has_side_effects=True, vmem_limit_bytes=56 * 2**20
        ),
        name="moe_layer",
    )(tok_f, tok_b, w_gate, w_up, w_down, pre_gate, pre_up, *routes)


def mix_kernel(rows, graded, *refs):
    block_f, block_b, tables = refs[:3]
    extra = 2 if graded else 0
    outs = refs[3 + extra : 5 + extra]
    stage, sems = refs[-2:]
    block_rows, width = block_f.shape
    chunks = block_rows // rows
    pad = padded(rows)
    unpack = selection(chunks, rows, pad)
    copies = []
    for k, block in enumerate((block_f, block_b)):
        weight = tables[k][:, :pad]
        high = narrow(weight)
        both = jnp.concatenate([high, narrow(weight - wide(high))], axis=1)
        full = narrow(dot(unpack, block[...]))
        for j in range(chunks):
            part = full[j * pad : (j + 1) * pad]
            cols = pl.ds(j * width, width)
            stage[k, :, cols] = narrow(dot(both, jnp.concatenate([part, part], axis=0)))
            copies.append(
                pltpu.make_async_copy(
                    stage.at[k, :, cols], outs[k].at[:, cols], sems.at[k * chunks + j]
                )
            )
            copies[-1].start()
    if graded:
        dots, ids = refs[3], refs[4]
        slots = slot_table(ids[...], rows)
        found = jnp.sum(slots * dots[:1], axis=1, keepdims=True)
        refs[7][...] = jnp.where(ids[...] == 0, found, 0.0)
    for copy in copies:
        copy.wait()


def mix(block_f, block_b, tables, rows, grading):
    block_rows, width = block_f.shape
    tokens = tables.shape[1]
    chunks = block_rows // rows
    vmem = pl.BlockSpec(memory_space=pltpu.VMEM)
    anywhere = pl.BlockSpec(memory_space=pl.ANY)
    shape = jax.ShapeDtypeStruct((tokens, chunks * width), jnp.bfloat16)
    out_shape = [shape, shape]
    if grading:
        out_shape.append(jax.ShapeDtypeStruct(grading[1].shape, jnp.float32))
    return pl.pallas_call(
        functools.partial(mix_kernel, rows, bool(grading)),
        out_shape=tuple(out_shape),
        in_specs=[vmem] * (3 + len(grading)),
        out_specs=tuple([anywhere, anywhere] + [vmem] * (len(out_shape) - 2)),
        scratch_shapes=[
            pltpu.VMEM((2, tokens, chunks * width), jnp.bfloat16),
            pltpu.SemaphoreType.DMA((2 * chunks,)),
        ],
        name="mix",
    )(block_f, block_b, tables, *grading)


def body(
    act_in,
    cotangent,
    fwd_ids,
    fwd_gates,
    bwd_ids,
    bwd_gates,
    gate_w,
    up_w,
    down_w,
    gate_pre,
    up_pre,
):
    ndev = lax.axis_size("expert")
    ff_dev = gate_w.shape[2]
    slices = FF // ff_dev
    experts = ndev // slices
    capacity = gate_pre.shape[1] // ndev
    rows = experts * capacity
    weights = (gate_w[0], up_w[0], down_w[0])

    if experts == 1:
        routes = (fwd_ids[0], fwd_gates[0], bwd_ids[0], bwd_gates[0])
        block_f, block_b, dots, tables = run_layer(
            act_in[0], cotangent[0], *weights, gate_pre[0], up_pre[0], routes, slices, rows
        )
        outs = mix(block_f, block_b, tables, rows, (dots, bwd_ids[0]))
        return tuple(out[None] for out in outs)

    chunks = 16 // math.gcd(16, rows)
    features = act_in.shape[2]
    width = features // chunks
    columns = [[g * slices + i for g in range(experts)] for i in range(slices)]

    def exchange(value):
        return lax.all_to_all(
            value, "expert", split_axis=0, concat_axis=0, axis_index_groups=columns, tiled=True
        )

    matches_f, placing_f, weights_f = routing(fwd_ids[0], fwd_gates[0], experts, capacity)
    matches_b, placing_b, weights_b = routing(bwd_ids[0], bwd_gates[0], experts, capacity)

    def prepare(tokens, placing):
        chosen = placing.reshape(rows, tokens.shape[0])
        picked = dot(chosen.astype(jnp.bfloat16), tokens).astype(jnp.bfloat16)
        picked = exchange(picked.reshape(experts, capacity, features))
        return picked.reshape(rows, features)

    def by_group(saved):
        saved = saved.reshape(experts, slices, capacity, ff_dev).transpose(1, 0, 2, 3)
        return saved.reshape(slices * rows, ff_dev)

    block_f, block_b, dots = run_layer(
        prepare(act_in[0], placing_f), prepare(cotangent[0], placing_b), *weights,
        by_group(gate_pre[0]), by_group(up_pre[0]), (), slices, rows,
    )
    mine = exchange(dots[0, :rows].reshape(experts, capacity))

    def send_back(block):
        table = block.reshape(chunks, rows, width).transpose(1, 0, 2)
        table = exchange(table.reshape(experts, capacity, features))
        table = table.reshape(rows, chunks, width).transpose(1, 0, 2)
        return table.reshape(chunks * rows, width)

    token_dots = jnp.sum(placing_b * mine[:, :, None], axis=1)
    gate_grad = jnp.sum(jnp.where(matches_b, token_dots[:, :, None], 0.0), axis=0)

    def weight_table(placing, weights):
        table = (placing * weights[:, None, :]).reshape(rows, -1).T
        return jnp.pad(table, ((0, 0), (0, LANES - rows)))

    def onward(block, placing, weights, step):
        block = from_behind(send_back(block), "section", step)
        return block, from_behind(weight_table(placing, weights), "section", step)

    block_f, table_f = onward(block_f, placing_f, weights_f, 1)
    block_b, table_b = onward(block_b, placing_b, weights_b, -1)
    next_act, prev_grad = mix(block_f, block_b, jnp.stack([table_f, table_b]), rows, ())
    return (next_act[None], prev_grad[None], gate_grad[None])


def solution(mesh):
    in_specs = (
        P("section", "expert", None),
        P("section", "expert", None),
        P("section", "expert", None),
        P("section", "expert", None),
        P("section", "expert", None),
        P("section", "expert", None),
        P("section", None, "expert"),
        P("section", None, "expert"),
        P("section", "expert", None),
        P("section", None, "expert"),
        P("section", None, "expert"),
    )
    out_specs = (
        P("section", "expert", None),
        P("section", "expert", None),
        P("section", "expert", None),
    )
    return jax.shard_map(body, mesh=mesh, in_specs=in_specs, out_specs=out_specs, check_vma=False)
```

time: 121 us -> 112 us (0.926)
  Pallas kernels: 114 us -> 104 us
  local copies, waits for them, and re-layouts: 2.87 us -> 7.14 us
  other arithmetic: 2.42 us -> 0 us
    pallas_call x2, Pallas kernels: 114 us -> 104 us  [the longest x1 99.6 us: run_layer(): pl.pallas_call(functools.partial(layer_kernel, slices, chunks, rows, hop)...]
    unnamed x4 -> x5, local copies, waits for them, and re-layouts: 0.68 us -> 7.14 us
    reduce_sum x5 -> x0, other arithmetic: 1.74 us -> none  [the longest x2 1.44 us: routing(): weights = jnp.sum(jnp.where(matches, gates[None, :, :], 0.0), axis=2)]
    another operation x10 -> x0, local copies, waits for them, and re-layouts: 1.49 us -> none  [the longest x4 1.26 us: prepare(): return (tokens, jnp.tile(chosen, (chunks, 1)))]
  transfers between devices with their start and end apart: 2 -> 0, of which waited for: 0 -> 0; matrix products, arithmetic and copies ran while one was open for 3% -> 0% of each run, Pallas kernels for 90% -> 0%
where the time goes in v1:
time: 112 us; the launch traced here: 111 us
  Pallas kernels  104 us (93%)
  local copies, waits for them, and re-layouts  7.14 us (6%)
    pallas_call x1, Pallas kernels, run_layer(): pl.pallas_call(functools.partial(layer_kernel, slices, chunks, rows, hop)...  99.6 us
    unnamed x5, local copies, waits for them, and re-layouts  7.14 us
    pallas_call x1, Pallas kernels, mix(): pl.pallas_call(functools.partial(mix_kernel, rows, bool(grading)), out_sh...  4.02 us

profile of v1, /device:TPU:1, one launch (start us, length us, event | category | flops | bytes accessed | tf_op | source)
XLA Modules:
  0.0 111.4 jit_solution(1349196025939522754)
XLA Ops:
  0.6 1.4 %copy.14 = s32[1,128,8]{2,1,0:T(8,128)} copy(s32[1,128,8]{1,2,0:T(8,128)} %param.13) | data formatting | bytes 8192 | tf_op args[2]
  2.0 1.4 %copy.15 = f32[1,128,8]{2,1,0:T(8,128)} copy(f32[1,128,8]{1,2,0:T(8,128)} %param.14) | data formatting | bytes 8192 | tf_op args[3]
  3.5 1.4 %copy.16 = s32[1,128,8]{2,1,0:T(8,128)} copy(s32[1,128,8]{1,2,0:T(8,128)} %param.15) | data formatting | bytes 8192 | tf_op args[4]
  4.9 1.4 %copy.17 = f32[1,128,8]{2,1,0:T(8,128)} copy(f32[1,128,8]{1,2,0:T(8,128)} %param.16) | data formatting | bytes 8192 | tf_op args[5]
  6.3 99.6 %moe_layer.1 = (bf16[80,896]{1,0:T(8,128)(2,1)}, bf16[80,896]{1,0:T(8,128)(2,1)}, f32[8,128]{1,0:T(8,128)}, f32[2,128,128]{2,1,0:T(8,128)}) custom-call(bf16[128,7168]{1,0:T(8,128)(2,1)} %bitcast.14, bf16[128,7168]{1,0:T(8,128)(2,1)} %bitcast.15, bf16[7168,128]{1,0:T(8,128)(2,1)} %bitcast.16, bf16[7168,128]{1,0:T(8,128)(2,1)} %bitcast.17, ...), custom_call_target="tpu_custom_call" | custom-call | tf_op jit(solution)/shard_map/moe_layer/pallas_call | solution.py:433
  105.9 4.0 %mix.1 = (bf16[128,7168]{1,0:T(8,128)(2,1)}, bf16[128,7168]{1,0:T(8,128)(2,1)}, f32[128,8]{1,0:T(8,128)}) custom-call(bf16[80,896]{1,0:T(8,128)(2,1)} %get-tuple-element.10.refs_0_, bf16[80,896]{1,0:T(8,128)(2,1)} %get-tuple-element.11.refs_1_, f32[2,128,128]{2,1,0:T(8,128)} %get-tuple-element.12.refs_2_, f32[8,128]{1,0:T(8,128)} %get-tuple-element.13.refs_3_, ...), custom_call_target="tpu_custom_call" | custom-call | tf_op jit(solution)/shard_map/mix/pallas_call | solution.py:513
  109.9 1.5 %copy.18 = f32[1,128,8]{1,2,0:T(8,128)} copy(f32[1,128,8]{2,1,0:T(8,128)} %bitcast.24) | data formatting | bytes 8192

commit v2 on v1

--- a/solution.py
+++ b/solution.py
@@ -74,17 +74,16 @@
     return narrow(jnp.where(chosen, 1.0, 0.0))
 
 
-def slot_table(ids, rows):
-    tokens = ids.shape[0]
-    hit = jnp.where(ids == 0, 1.0, 0.0)
-    routed = jnp.max(hit, axis=1, keepdims=True)
-    spread = jnp.broadcast_to(routed, (tokens, LANES))
+def slot_rows(ids, count):
+    tokens = ids.shape[1]
+    routed = jnp.max(jnp.where(ids == 0, 1.0, 0.0), axis=0, keepdims=True)
+    spread = jnp.broadcast_to(routed, (count, tokens))
     row = lax.broadcasted_iota(jnp.int32, (tokens, tokens), 0)
     column = lax.broadcasted_iota(jnp.int32, (tokens, tokens), 1)
-    lower = narrow(jnp.where(column <= row, 1.0, 0.0))
-    rank = dot(lower, narrow(spread)) - 1.0
-    lane = wide(lax.broadcasted_iota(jnp.int32, (tokens, LANES), 1))
-    return jnp.where((rank == lane) & (spread > 0.0), 1.0, 0.0)
+    upper = narrow(jnp.where(row <= column, 1.0, 0.0))
+    rank = dot(narrow(spread), upper) - 1.0
+    slot = wide(lax.broadcasted_iota(jnp.int32, (count, tokens), 0))
+    return jnp.where((rank == slot) & (spread > 0.0), 1.0, 0.0)
 
 
 class Links:
@@ -185,10 +184,10 @@
                 jnp.where(same == lax.broadcasted_iota(jnp.int32, shape, 1), 1.0, 0.0)
             )
         ids = routes[2 * mb][...]
-        slots = slot_table(ids, rows)
+        slots = slot_rows(ids, LANES)
         gates = jnp.where(ids == 0, routes[2 * mb + 1][...], 0.0)
-        table[mb] = slots * jnp.sum(gates, axis=1, keepdims=True)
-        return narrow(jnp.transpose(slots)[:pad])
+        table[mb] = jnp.transpose(slots * jnp.sum(gates, axis=0, keepdims=True))
+        return narrow(slots[:pad])
 
     def place(mb, chosen, waits):
         for j in range(chunks):
@@ -291,13 +290,9 @@
             sig = 1.0 / (1.0 + jnp.exp(-gate))
             activated = gate * sig
             dots = jnp.sum(total * activated * up, axis=1, keepdims=True)
-            shape = (QUAD * pad, LANES)
-            inner = lax.broadcasted_iota(jnp.int32, shape, 0) & (pad - 1)
-            lane = lax.broadcasted_iota(jnp.int32, shape, 1)
-            placed = jnp.where(inner == lane, dots, 0.0)
             for b in range(QUAD):
-                line = jnp.sum(placed[b * pad : (b + 1) * pad], axis=0, keepdims=True)
-                dot_out[group + b] = jnp.broadcast_to(line, (8, LANES))
+                mine = dots[b * pad : (b + 1) * pad]
+                dot_out[group + b] = jnp.broadcast_to(mine, (pad, LANES))
             for copy in dots_sent[q]:
                 links.start(copy)
             grad_gate = narrow(total * up * sig * (1.0 + gate * (1.0 - sig)))
@@ -426,7 +421,7 @@
     out_shape = [
         jax.ShapeDtypeStruct(block, jnp.bfloat16),
         jax.ShapeDtypeStruct(block, jnp.bfloat16),
-        jax.ShapeDtypeStruct((8, LANES), jnp.float32),
+        jax.ShapeDtypeStruct((pad, LANES), jnp.float32),
     ]
     if hop:
         out_shape.append(jax.ShapeDtypeStruct(tables, jnp.float32))
@@ -453,8 +448,8 @@
             pltpu.VMEM((2,) + block, jnp.bfloat16),
             pltpu.VMEM(tables, jnp.float32),
             pltpu.VMEM(tables, jnp.float32),
-            pltpu.VMEM((slices, 8, LANES), jnp.float32),
-            pltpu.VMEM((slices, 8, LANES), jnp.float32),
+            pltpu.VMEM((slices, pad, LANES), jnp.float32),
+            pltpu.VMEM((slices, pad, LANES), jnp.float32),
             pltpu.SemaphoreType.DMA((5 * chunks,)),
             pltpu.SemaphoreType.DMA((SEMAPHORES,)),
             pltpu.SemaphoreType.DMA((SEMAPHORES,)),
@@ -493,8 +488,8 @@
             copies[-1].start()
     if graded:
         dots, ids = refs[3], refs[4]
-        slots = slot_table(ids[...], rows)
-        found = jnp.sum(slots * dots[:1], axis=1, keepdims=True)
+        slots = slot_rows(ids[...], pad)
+        found = jnp.sum(slots * dots[...], axis=0, keepdims=True)
         refs[7][...] = jnp.where(ids[...] == 0, found, 0.0)
     for copy in copies:
         copy.wait()
@@ -545,12 +540,12 @@
     weights = (gate_w[0], up_w[0], down_w[0])
 
     if experts == 1:
-        routes = (fwd_ids[0], fwd_gates[0], bwd_ids[0], bwd_gates[0])
+        routes = tuple(each[0].T for each in (fwd_ids, fwd_gates, bwd_ids, bwd_gates))
         block_f, block_b, dots, tables = run_layer(
             act_in[0], cotangent[0], *weights, gate_pre[0], up_pre[0], routes, slices, rows
         )
-        outs = mix(block_f, block_b, tables, rows, (dots, bwd_ids[0]))
-        return tuple(out[None] for out in outs)
+        next_act, prev_grad, grads = mix(block_f, block_b, tables, rows, (dots, routes[2]))
+        return (next_act[None], prev_grad[None], grads.T[None])
 
     chunks = 16 // math.gcd(16, rows)
     features = act_in.shape[2]
@@ -579,7 +574,7 @@
         prepare(act_in[0], placing_f), prepare(cotangent[0], placing_b), *weights,
         by_group(gate_pre[0]), by_group(up_pre[0]), (), slices, rows,
     )
-    mine = exchange(dots[0, :rows].reshape(experts, capacity))
+    mine = exchange(dots[:rows, 0].reshape(experts, capacity))
 
     def send_back(block):
         table = block.reshape(chunks, rows, width).transpose(1, 0, 2)

time: 112 us -> 105 us (0.938)
  local copies, waits for them, and re-layouts: 7.14 us -> 0 us
    unnamed x5 -> x0, local copies, waits for them, and re-layouts: 7.14 us -> none
where the time goes in v2:
time: 105 us
  Pallas kernels  104 us (99%)
    pallas_call x1, Pallas kernels, run_layer(): pl.pallas_call(functools.partial(layer_kernel, slices, chunks, rows, hop)...  100 us
    pallas_call x1, Pallas kernels, mix(): pl.pallas_call(functools.partial(mix_kernel, rows, bool(grading)), out_sh...  3.98 us

profile of v2, /device:TPU:1, one launch (start us, length us, event | category | flops | bytes accessed | tf_op | source)
XLA Modules:
  0.0 105.2 jit_solution(8353306935374436097)
XLA Ops:
  0.6 100.4 %moe_layer.1 = (bf16[80,896]{1,0:T(8,128)(2,1)}, bf16[80,896]{1,0:T(8,128)(2,1)}, f32[16,128]{1,0:T(8,128)}, f32[2,128,128]{2,1,0:T(8,128)}) custom-call(bf16[128,7168]{1,0:T(8,128)(2,1)} %bitcast.24, bf16[128,7168]{1,0:T(8,128)(2,1)} %bitcast.25, bf16[7168,128]{1,0:T(8,128)(2,1)} %bitcast.26, bf16[7168,128]{1,0:T(8,128)(2,1)} %bitcast.27, ...), custom_call_target="tpu_custom_call" | custom-call | tf_op jit(solution)/shard_map/moe_layer/pallas_call | solution.py:428
  101.0 4.0 %mix.1 = (bf16[128,7168]{1,0:T(8,128)(2,1)}, bf16[128,7168]{1,0:T(8,128)(2,1)}, f32[8,128]{1,0:T(8,128)}) custom-call(bf16[80,896]{1,0:T(8,128)(2,1)} %get-tuple-element.10.refs_0_, bf16[80,896]{1,0:T(8,128)(2,1)} %get-tuple-element.11.refs_1_, f32[2,128,128]{2,1,0:T(8,128)} %get-tuple-element.12.refs_2_, f32[16,128]{1,0:T(8,128)} %get-tuple-element.13.refs_3_, ...), custom_call_target="tpu_custom_call" | custom-call | tf_op jit(solution)/shard_map/mix/pallas_call | solution.py:508

commit v3 on v2

--- a/solution.py
+++ b/solution.py
@@ -11,11 +11,29 @@
 FF = 2048
 QUAD = 4
 LANES = 128
-AHEAD = 3
-SECOND_LAG = 1
-THIRD_LAG = 2
-SEMAPHORES = 128
+SEMAPHORES = 160
+TABLES_AFTER = "fwd 0 B"
 MESH = pl.DeviceIdType.MESH
+
+SCHEDULE = (
+    "place 0", "zs 0 2", "own 0 B", "place 1", "zs 1 1", "own 1 0", "own 1 B", "zs 0 1",
+    "zs 0 3", "zs 1 2", "own 0 0", "fwd 1 0", "own 0 2", "own 1 1", "fwd 0 0", "own 0 3",
+    "fwd 1 B", "zs 1 3", "fwd 0 B", "fwd 1 1", "own 0 1", "fwd 0 2", "own 1 2", "zB 0 1",
+    "zB 0 2", "zB 0 3", "fwd 0 3", "comp 0 0", "zB 1 2", "fwd 1 2", "fwd 0 1", "zB 1 3",
+    "own 1 3", "comp 0 2", "comp 0 3", "fwd 1 3", "comp 0 1", "sec 0 2", "comp 1 2", "sec 0 3",
+    "zB 1 1", "thi 0 2", "comp 1 3", "sec 0 1", "sec 1 2", "sumB 0", "comp 1 1", "thi 0 3",
+    "sec 1 3", "thi 0 1", "sec 1 1", "comp 1 0", "thi 1 2", "sec 0 0", "thi 1 3", "thi 1 1",
+    "sec 0 B", "sumB 1", "sec 1 0", "thi 0 B", "sec 1 B", "thi 1 B", "thi 0 0", "thi 1 0",
+    "fin 0", "fin 1", "del 0", "del 1",
+)
+GATHER_X = (
+    {"B": True, 0: False, 1: False, 2: True, 3: False},
+    {"B": True, 0: True, 1: False, 2: False, 3: False},
+)
+REDUCE_X = (
+    {"B": True, 0: True, 1: True, 2: True, 3: True},
+    {"B": False, 0: True, 1: False, 2: False, 3: True},
+)
 
 
 def from_behind(value, axis, steps):
@@ -118,8 +136,9 @@
     outs = 4 if hop else 3
     out_f, out_b, out_dots = refs[inputs : inputs + 3]
     (
-        tok, wc, wd, gat, par, xb, yb, pre, rs1, rs2, rsz, hold, hold2, sums, landed, table,
-        table_got, dot_out, dot_in, local_sems, send_sems, recv_sems,
+        tok, wc, wd, gat_a, gat_b, par_a, par_b, xb, yb, pre, rs1, rs2, rsz, hold, hold2, zgot_b,
+        sum_b, rs1_b, rs2_b, hold_b, sums, landed, table, table_got, dot_out, dot_in, local_sems,
+        send_sems, recv_sems,
     ) = refs[inputs + outs :]
     device = lax.axis_index("expert")
     me = device % slices
@@ -133,6 +152,7 @@
     features, ff = wc.shape[0], wd.shape[0]
     width = features // chunks
     pad = padded(rows)
+    cut = gat_a.shape[3]
 
     def bid(q, mask):
         return xor(z, q) * QUAD + xor(lo, mask)
@@ -166,12 +186,15 @@
             pl.semaphore_signal(barrier, inc=1, device_id={"section": peer}, device_id_type=MESH)
         greeted += 2
 
-    load_b = [load(tok_b.at[:, cols_of(j)], tok.at[1, :, cols_of(j)]) for j in range(chunks)]
-    load_w = []
-    for j in range(chunks):
-        load_w.append(load(w_gate.at[cols_of(j), :], wc.at[cols_of(j), pl.ds(0, ff)]))
-        load_w.append(load(w_up.at[cols_of(j), :], wc.at[cols_of(j), pl.ds(ff, ff)]))
-        load_w.append(load(w_down.at[:, cols_of(j)], wd.at[:, cols_of(j)]))
+    load_b, load_w = [], []
+
+    def start_loads():
+        for j in range(chunks):
+            load_b.append(load(tok_b.at[:, cols_of(j)], tok.at[1, :, cols_of(j)]))
+        for j in range(chunks):
+            load_w.append(load(w_gate.at[cols_of(j), :], wc.at[cols_of(j), pl.ds(0, ff)]))
+            load_w.append(load(w_up.at[cols_of(j), :], wc.at[cols_of(j), pl.ds(ff, ff)]))
+            load_w.append(load(w_down.at[:, cols_of(j)], wd.at[:, cols_of(j)]))
 
     unpack = selection(chunks, rows, pad)
     pack = selection(chunks, rows, pad, flip=True)
@@ -184,55 +207,63 @@
                 jnp.where(same == lax.broadcasted_iota(jnp.int32, shape, 1), 1.0, 0.0)
             )
         ids = routes[2 * mb][...]
-        slots = slot_rows(ids, LANES)
-        gates = jnp.where(ids == 0, routes[2 * mb + 1][...], 0.0)
-        table[mb] = jnp.transpose(slots * jnp.sum(gates, axis=0, keepdims=True))
-        return narrow(slots[:pad])
+        return narrow(slot_rows(ids, pad))
+
+    def send_tables():
+        for mb in range(2):
+            ids = routes[2 * mb][...]
+            gates = jnp.where(ids == 0, routes[2 * mb + 1][...], 0.0)
+            weighted = slot_rows(ids, LANES) * jnp.sum(gates, axis=0, keepdims=True)
+            table[mb] = jnp.transpose(weighted)
+            links.start(tables[mb])
 
     def place(mb, chosen, waits):
         for j in range(chunks):
             waits[j].wait()
+            if mb == 0 and j == chunks - 1:
+                start_loads()
             picked = dot(chosen, tok[mb, :, cols_of(j)])
             yb[0, pl.ds(j * pad, pad), :] = narrow(picked)
-        gat[mb, me] = narrow(dot(pack, yb[0]))
+        packed = narrow(dot(pack, yb[0]))
+        gat_a[mb, me] = packed[:, :cut]
+        gat_b[mb, me] = packed[:, cut:]
 
     links = Links(send_sems, recv_sems)
-
-    order = list(range(1, depth)) + [0]
-    steps = [(0, q) for q in range(depth)] + [(1, q) for q in order]
-    tiles = width // LANES
-    cut = tiles // 2 * LANES
-    zsend, parts = {}, {}
-    own_x, own_y, forward = {}, {}, {}
-    r1, r2, rz, dots_sent = {}, {}, {}, {}
-    for step in steps:
-        mb, q = step
-        if step == steps[-1]:
-            parts[step] = [(True, pl.ds(0, cut)), (False, pl.ds(cut, width - cut))]
-        else:
-            parts[step] = [(q % 2 == 0, pl.ds(0, width))]
-        if q > 0:
-            zsend[step] = links.copy(gat.at[mb, me], gat.at[mb, me], zp[q])
-            rz[step] = links.copy(hold2.at[mb, q], rsz.at[mb, q], zp[q])
-        own_x[step], own_y[step], forward[step], r1[step], r2[step] = [], [], [], [], []
-        for first, cols in parts[step]:
-            block = gat.at[mb, bid(q, 0), :, cols]
-            own_x[step].append(links.copy(block, block, xp))
-            own_y[step].append(links.copy(block, block, yp))
-            got = gat.at[mb, bid(q, 2 if first else 1), :, cols]
-            forward[step].append(links.copy(got, got, xp if first else yp))
-            m1, p1, p2 = (1, xp, yp) if first else (2, yp, xp)
-            r1[step].append([
-                links.copy(par.at[mb, bid(q, 3), :, cols], rs1.at[mb, q, 1, :, cols], p1),
-                links.copy(par.at[mb, bid(q, m1), :, cols], rs1.at[mb, q, 0, :, cols], p1),
-            ])
-            r2[step].append(links.copy(hold.at[mb, q, :, cols], rs2.at[mb, q, :, cols], p2))
-        if mb == 1:
-            dots_sent[q] = [
-                links.copy(dot_out.at[bid(q, m)], dot_in.at[q * QUAD + m], base + bid(q, m))
-                for m in range(QUAD)
-                if q or m
-            ]
+    offsets = range(1, depth)
+    own_x, own_y, forward, r1, r2 = {}, {}, {}, {}, {}
+    zsend, rz, bsend, rb, dots_sent = {}, {}, {}, {}, {}
+    for mb in range(2):
+        for q in offsets:
+            zsend[mb, q] = links.copy(gat_a.at[mb, me], gat_a.at[mb, me], zp[q])
+            rz[mb, q] = links.copy(hold2.at[mb, q], rsz.at[mb, q], zp[q])
+            quad = gat_b.at[mb, pl.ds(z * QUAD, QUAD)]
+            bsend[mb, q] = links.copy(quad, quad, zp[q])
+            theirs = par_b.at[mb, pl.ds(xor(z, q) * QUAD, QUAD)]
+            rb[mb, q] = links.copy(theirs, zgot_b.at[mb, q], zp[q])
+        for step in ["B"] + list(range(depth)):
+            at = (mb, step)
+            q, gat = (0, gat_b) if step == "B" else (step, gat_a)
+            block = gat.at[mb, bid(q, 0)]
+            own_x[at] = links.copy(block, block, xp)
+            own_y[at] = links.copy(block, block, yp)
+            via_x = GATHER_X[mb][step]
+            got = gat.at[mb, bid(q, 2 if via_x else 1)]
+            forward[at] = links.copy(got, got, xp if via_x else yp)
+            m1, p1, p2 = (1, xp, yp) if REDUCE_X[mb][step] else (2, yp, xp)
+            if step == "B":
+                far, near = sum_b.at[mb, xor(lo, 3)], sum_b.at[mb, xor(lo, m1)]
+                got1, held, got2 = rs1_b.at[mb], hold_b.at[mb], rs2_b.at[mb]
+            else:
+                far, near = par_a.at[mb, bid(q, 3)], par_a.at[mb, bid(q, m1)]
+                got1, held, got2 = rs1.at[mb, q], hold.at[mb, q], rs2.at[mb, q]
+            r1[at] = [links.copy(far, got1.at[1], p1), links.copy(near, got1.at[0], p1)]
+            r2[at] = links.copy(held, got2, p2)
+    for q in range(depth):
+        dots_sent[q] = [
+            links.copy(dot_out.at[bid(q, m)], dot_in.at[q * QUAD + m], base + bid(q, m))
+            for m in range(QUAD)
+            if q or m
+        ]
     if hop:
         across = [
             links.copy(sums.at[0], landed.at[0], ahead, "section"),
@@ -243,33 +274,63 @@
             links.copy(table.at[1], table_got.at[1], behind, "section"),
         ]
 
-    def do_own(step):
-        if step[1] > 0:
-            zsend[step].wait_recv()
-        for copy_x, copy_y in zip(own_x[step], own_y[step]):
-            links.start(copy_x)
-            links.start(copy_y)
-
-    def start_mb(mb):
-        for q in range(1, depth):
-            links.start(zsend[mb, q])
-
-    def do_forward(step):
-        for k, (first, cols) in enumerate(parts[step]):
-            (own_y if first else own_x)[step][k].wait_recv()
-            links.start(forward[step][k])
-
-    def compute(step):
-        mb, q = step
-        for k, (first, cols) in enumerate(parts[step]):
-            (own_x if first else own_y)[step][k].wait_recv()
-            forward[step][k].wait_recv()
+    arrived = []
+
+    def await_all(*copies):
+        for copy in copies:
+            if not any(copy is done for done in arrived):
+                arrived.append(copy)
+                copy.wait_recv()
+
+    def do_place(mb):
+        place(mb, choose(mb), load_b if mb else load_f)
+        if mb == 0:
+            pl.semaphore_wait(barrier, greeted)
+
+    def do_zs(mb, q):
+        links.start(zsend[mb, q])
+
+    def do_own(mb, step):
+        if step != "B" and step > 0:
+            await_all(zsend[mb, step])
+        links.start(own_x[mb, step])
+        links.start(own_y[mb, step])
+
+    def do_fwd(mb, step):
+        await_all((own_y if GATHER_X[mb][step] else own_x)[mb, step])
+        links.start(forward[mb, step])
+
+    def await_quad(mb, step):
+        await_all(own_x[mb, step], own_y[mb, step], forward[mb, step])
+
+    def do_bsend(mb, q):
+        await_quad(mb, "B")
+        links.start(bsend[mb, q])
+
+    ready = []
+
+    def do_compute(mb, q):
+        await_quad(mb, q)
+        if q > 0:
+            await_all(bsend[mb, q])
+        else:
+            await_quad(mb, "B")
+        if not ready:
+            ready.append(True)
+            for copy in load_w:
+                copy.wait()
+            spaced = selection(slices, rows, pad)
+            for k, saved in enumerate((pre_gate, pre_up)):
+                pre[k] = narrow(dot(spaced, saved[...])).reshape(pre.shape[1:])
         zq = xor(z, q)
         group = zq * QUAD
         for b in range(QUAD):
-            full = narrow(dot(unpack, gat[mb, group + b]))
+            full_a = narrow(dot(unpack, gat_a[mb, group + b]))
+            full_b = narrow(dot(unpack, gat_b[mb, group + b]))
             for j in range(chunks):
-                xb[pl.ds(b * pad, pad), cols_of(j)] = full[j * pad : (j + 1) * pad]
+                piece_rows = slice(j * pad, (j + 1) * pad)
+                xb[pl.ds(b * pad, pad), pl.ds(j * width, cut)] = full_a[piece_rows]
+                xb[pl.ds(b * pad, pad), pl.ds(j * width + cut, width - cut)] = full_b[piece_rows]
         total = None
         for j in range(chunks):
             if mb == 0:
@@ -293,8 +354,6 @@
             for b in range(QUAD):
                 mine = dots[b * pad : (b + 1) * pad]
                 dot_out[group + b] = jnp.broadcast_to(mine, (pad, LANES))
-            for copy in dots_sent[q]:
-                links.start(copy)
             grad_gate = narrow(total * up * sig * (1.0 + gate * (1.0 - sig)))
             both = jnp.concatenate([grad_gate, narrow(total * activated)], axis=1)
 
@@ -306,100 +365,101 @@
             for b in range(QUAD):
                 yb[b, pl.ds(j * pad, pad), :] = full[b * pad : (b + 1) * pad]
         for b in range(QUAD):
-            par[mb, group + b] = narrow(dot(pack, yb[b]))
-        for copies in r1[step]:
-            for copy in copies:
+            packed = narrow(dot(pack, yb[b]))
+            par_a[mb, group + b] = packed[:, :cut]
+            par_b[mb, group + b] = packed[:, cut:]
+        if q > 0:
+            links.start(rb[mb, q])
+        for copy in r1[mb, q]:
+            links.start(copy)
+        if mb == 1:
+            for copy in dots_sent[q]:
                 links.start(copy)
 
-    def second(step):
-        mb, q = step
-        for k, (first, cols) in enumerate(parts[step]):
-            r1[step][k][0].wait_recv()
-            m2 = 2 if first else 1
-            total = wide(par[mb, bid(q, m2), :, cols]) + wide(rs1[mb, q, 1, :, cols])
-            hold[mb, q, :, cols] = narrow(total)
-            links.start(r2[step][k])
-
-    def third(step):
-        mb, q = step
-        for k, (first, cols) in enumerate(parts[step]):
-            r1[step][k][1].wait_recv()
-            r2[step][k].wait_recv()
-            total = wide(par[mb, bid(q, 0), :, cols]) + wide(rs1[mb, q, 0, :, cols])
-            total = total + wide(rs2[mb, q, :, cols])
-            hold2[mb, q, :, cols] = narrow(total)
-        if q > 0:
-            links.start(rz[step])
-
-    def finish(mb):
+    def do_gather_b(mb):
+        total = wide(par_b[mb, pl.ds(z * QUAD, QUAD)])
+        for q in offsets:
+            await_all(rb[mb, q])
+            total = total + wide(zgot_b[mb, q])
+        sum_b[mb] = narrow(total)
+        for copy in r1[mb, "B"]:
+            links.start(copy)
+
+    def shares(mb, step):
+        if step == "B":
+            return (lambda m: sum_b[mb, xor(lo, m)]), rs1_b.at[mb], hold_b.at[mb], rs2_b.at[mb]
+        q = step
+        return (lambda m: par_a[mb, bid(q, m)]), rs1.at[mb, q], hold.at[mb, q], rs2.at[mb, q]
+
+    def do_second(mb, step):
+        mine, got, held, unused = shares(mb, step)
+        await_all(r1[mb, step][0])
+        held[...] = narrow(wide(mine(2 if REDUCE_X[mb][step] else 1)) + wide(got[1]))
+        links.start(r2[mb, step])
+
+    def do_third(mb, step):
+        mine, got, unused, got2 = shares(mb, step)
+        await_all(r1[mb, step][1], r2[mb, step])
+        total = narrow(wide(mine(0)) + wide(got[0]) + wide(got2[...]))
+        if step == "B":
+            sums[mb, :, pl.ds(cut, width - cut)] = total
+        else:
+            hold2[mb, step] = total
+            if step > 0:
+                links.start(rz[mb, step])
+
+    def do_finish(mb):
         total = wide(hold2[mb, 0])
-        for q in range(1, depth):
-            rz[mb, q].wait_recv()
+        for q in offsets:
+            await_all(rz[mb, q])
             total = total + wide(rsz[mb, q])
-        sums[mb] = narrow(total)
+        sums[mb, :, pl.ds(0, cut)] = narrow(total)
         if hop:
             links.start(across[mb])
 
-    def deliver(mb, out):
+    def do_deliver(mb):
+        out = (out_f, out_b)[mb]
+        if mb == 1:
+            found = dot_out[me]
+            for q, m in peers:
+                copy = links_to[q, m]
+                await_all(copy)
+                found = found + dot_in[q * QUAD + m]
+            out_dots[...] = found
+            if hop:
+                out_tables = refs[inputs + 3]
+                await_all(*tables)
+                out_tables[...] = table_got[...]
         if hop:
-            across[mb].wait_recv()
+            await_all(across[mb])
             out[...] = landed[mb]
         else:
             out[...] = sums[mb]
 
-    place(0, choose(0), load_f)
-    pl.semaphore_wait(barrier, greeted)
-    do_own(steps[0])
-    start_mb(0)
-    place(1, choose(1), load_b)
-    start_mb(1)
-    if hop:
-        for copy in tables:
-            links.start(copy)
-    spaced = selection(slices, rows, pad)
-    for k, saved in enumerate((pre_gate, pre_up)):
-        pre[k] = narrow(dot(spaced, saved[...])).reshape(pre.shape[1:])
-
-    count = len(steps)
-    gathers = [(do_own, s) for s in range(1)]
-    for s in range(1, count):
-        gathers += [(do_own, s), (do_forward, s - 1)]
-    gathers = gathers[1:] + [(do_forward, count - 1)]
-
-    def gather_to(s):
-        while gathers and (do_forward, min(s, count - 1)) in gathers:
-            event, at = gathers.pop(0)
-            event(steps[at])
-
-    for t in range(count + THIRD_LAG):
-        gather_to(t + AHEAD - 1)
-        if t == 0:
-            for copy in load_w:
-                copy.wait()
-        if t < count:
-            compute(steps[t])
-        if 0 <= t - SECOND_LAG < count:
-            second(steps[t - SECOND_LAG])
-        if 0 <= t - THIRD_LAG < count:
-            third(steps[t - THIRD_LAG])
-        if t == count - 1:
-            finish(0)
-        if t == count:
-            deliver(0, out_f)
-    total = dot_out[me]
+    links_to = {}
     for q in range(depth):
-        for copy in dots_sent[q]:
-            copy.wait_recv()
-    for q, m in peers:
-        total = total + dot_in[q * QUAD + m]
-    out_dots[...] = total
-    if hop:
-        out_tables = refs[inputs + 3]
-        for k in range(2):
-            tables[k].wait_recv()
-            out_tables[k] = table_got[k]
-    finish(1)
-    deliver(1, out_b)
+        masks = [m for m in range(QUAD) if q or m]
+        for m, copy in zip(masks, dots_sent[q]):
+            links_to[q, m] = copy
+
+    events = {
+        "place": do_place,
+        "zs": do_zs,
+        "own": do_own,
+        "fwd": do_fwd,
+        "zB": do_bsend,
+        "comp": do_compute,
+        "sumB": do_gather_b,
+        "sec": do_second,
+        "thi": do_third,
+        "fin": do_finish,
+        "del": do_deliver,
+    }
+    for entry in SCHEDULE:
+        event, *at = entry.split()
+        events[event](*(step if step == "B" else int(step) for step in at))
+        if entry == TABLES_AFTER and hop:
+            send_tables()
     for copy in links.sent:
         copy.wait_send()
 
@@ -417,6 +477,8 @@
     vmem = pl.BlockSpec(memory_space=pltpu.VMEM)
     anywhere = pl.BlockSpec(memory_space=pl.ANY)
     block = (chunks * rows, width)
+    last = max(width // LANES // 7, 1) * LANES
+    part_a, part_b = (chunks * rows, width - last), (chunks * rows, last)
     tables = (2, tok_f.shape[0] if hop else 8, LANES)
     out_shape = [
         jax.ShapeDtypeStruct(block, jnp.bfloat16),
@@ -434,16 +496,23 @@
             pltpu.VMEM((2,) + tok_f.shape, jnp.bfloat16),
             pltpu.VMEM((features, 2 * ff), jnp.bfloat16),
             pltpu.VMEM((ff, features), jnp.bfloat16),
-            pltpu.VMEM((2, slices) + block, jnp.bfloat16),
-            pltpu.VMEM((2, slices) + block, jnp.bfloat16),
+            pltpu.VMEM((2, slices) + part_a, jnp.bfloat16),
+            pltpu.VMEM((2, slices) + part_b, jnp.bfloat16),
+            pltpu.VMEM((2, slices) + part_a, jnp.bfloat16),
+            pltpu.VMEM((2, slices) + part_b, jnp.bfloat16),
             pltpu.VMEM((group, features), jnp.bfloat16),
             pltpu.VMEM((QUAD, chunks * pad, width), jnp.bfloat16),
             pltpu.VMEM((2, depth, group, ff), jnp.bfloat16),
-            pltpu.VMEM((2, depth, 2) + block, jnp.bfloat16),
-            pltpu.VMEM((2, depth) + block, jnp.bfloat16),
-            pltpu.VMEM((2, depth) + block, jnp.bfloat16),
-            pltpu.VMEM((2, depth) + block, jnp.bfloat16),
-            pltpu.VMEM((2, depth) + block, jnp.bfloat16),
+            pltpu.VMEM((2, depth, 2) + part_a, jnp.bfloat16),
+            pltpu.VMEM((2, depth) + part_a, jnp.bfloat16),
+            pltpu.VMEM((2, depth) + part_a, jnp.bfloat16),
+            pltpu.VMEM((2, depth) + part_a, jnp.bfloat16),
+            pltpu.VMEM((2, depth) + part_a, jnp.bfloat16),
+            pltpu.VMEM((2, depth, QUAD) + part_b, jnp.bfloat16),
+            pltpu.VMEM((2, QUAD) + part_b, jnp.bfloat16),
+            pltpu.VMEM((2, 2) + part_b, jnp.bfloat16),
+            pltpu.VMEM((2,) + part_b, jnp.bfloat16),
+            pltpu.VMEM((2,) + part_b, jnp.bfloat16),
             pltpu.VMEM((2,) + block, jnp.bfloat16),
             pltpu.VMEM((2,) + block, jnp.bfloat16),
             pltpu.VMEM(tables, jnp.float32),

time: 105 us -> 90.4 us (0.86)
  Pallas kernels: 104 us -> 89.4 us
    pallas_call x1, Pallas kernels: 100 us -> 85.4 us  [run_layer(): pl.pallas_call(functools.partial(layer_kernel, slices, chunks, rows, hop)...]
where the time goes in v3:
time: 90.4 us; the launch traced here: 90.2 us
  Pallas kernels  89.4 us (99%)
    pallas_call x1, Pallas kernels, run_layer(): pl.pallas_call(functools.partial(layer_kernel, slices, chunks, rows, hop)...  85.4 us
    pallas_call x1, Pallas kernels, mix(): pl.pallas_call(functools.partial(mix_kernel, rows, bool(grading)), out_sh...  3.99 us

profile of v3, /device:TPU:1, one launch (start us, length us, event | category | flops | bytes accessed | tf_op | source)
XLA Modules:
  0.0 90.2 jit_solution(16091024321360472444)
XLA Ops:
  0.6 85.4 %moe_layer.1 = (bf16[80,896]{1,0:T(8,128)(2,1)}, bf16[80,896]{1,0:T(8,128)(2,1)}, f32[16,128]{1,0:T(8,128)}, f32[2,128,128]{2,1,0:T(8,128)}) custom-call(bf16[128,7168]{1,0:T(8,128)(2,1)} %bitcast.24, bf16[128,7168]{1,0:T(8,128)(2,1)} %bitcast.25, bf16[7168,128]{1,0:T(8,128)(2,1)} %bitcast.26, bf16[7168,128]{1,0:T(8,128)(2,1)} %bitcast.27, ...), custom_call_target="tpu_custom_call" | custom-call | tf_op jit(solution)/shard_map/moe_layer/pallas_call | solution.py:490
  86.0 4.0 %mix.1 = (bf16[128,7168]{1,0:T(8,128)(2,1)}, bf16[128,7168]{1,0:T(8,128)(2,1)}, f32[8,128]{1,0:T(8,128)}) custom-call(bf16[80,896]{1,0:T(8,128)(2,1)} %get-tuple-element.10.refs_0_, bf16[80,896]{1,0:T(8,128)(2,1)} %get-tuple-element.11.refs_1_, f32[2,128,128]{2,1,0:T(8,128)} %get-tuple-element.12.refs_2_, f32[16,128]{1,0:T(8,128)} %get-tuple-element.13.refs_3_, ...), custom_call_target="tpu_custom_call" | custom-call | tf_op jit(solution)/shard_map/mix/pallas_call | solution.py:577

commit v4 on v3

--- a/solution.py
+++ b/solution.py
@@ -16,23 +16,27 @@
 MESH = pl.DeviceIdType.MESH
 
 SCHEDULE = (
-    "place 0", "zs 0 2", "own 0 B", "place 1", "zs 1 1", "own 1 0", "own 1 B", "zs 0 1",
-    "zs 0 3", "zs 1 2", "own 0 0", "fwd 1 0", "own 0 2", "own 1 1", "fwd 0 0", "own 0 3",
-    "fwd 1 B", "zs 1 3", "fwd 0 B", "fwd 1 1", "own 0 1", "fwd 0 2", "own 1 2", "zB 0 1",
-    "zB 0 2", "zB 0 3", "fwd 0 3", "comp 0 0", "zB 1 2", "fwd 1 2", "fwd 0 1", "zB 1 3",
-    "own 1 3", "comp 0 2", "comp 0 3", "fwd 1 3", "comp 0 1", "sec 0 2", "comp 1 2", "sec 0 3",
-    "zB 1 1", "thi 0 2", "comp 1 3", "sec 0 1", "sec 1 2", "sumB 0", "comp 1 1", "thi 0 3",
-    "sec 1 3", "thi 0 1", "sec 1 1", "comp 1 0", "thi 1 2", "sec 0 0", "thi 1 3", "thi 1 1",
-    "sec 0 B", "sumB 1", "sec 1 0", "thi 0 B", "sec 1 B", "thi 1 B", "thi 0 0", "thi 1 0",
-    "fin 0", "fin 1", "del 0", "del 1",
+    "place 0", "oy 0 B", "ox 0 0", "zs 0 2", "zs 0 1", "place 1", "oy 1 0", "zs 1 2", "ox 0 B",
+    "oy 1 B", "ox 1 0", "oy 0 0", "zs 1 1", "fwd 0 0", "ox 1 B", "fwd 0 B", "fwd 1 0",
+    "fwd 1 B", "ox 0 1", "oy 0 2", "oy 0 1", "zs 0 3", "ox 0 2", "zB 0 1", "comp 0 0", "zB 1 1",
+    "ox 1 1", "oy 1 2", "ox 1 2", "comp 1 0", "fwd 0 2", "zB 0 2", "fwd 1 2", "oy 0 3",
+    "fwd 0 1", "zB 1 2", "ox 0 3", "oy 1 1", "zB 0 3", "zs 1 3", "fwd 1 1", "comp 0 2",
+    "rf 0 2", "zB 1 3", "fwd 0 3", "rn 0 2", "comp 1 2", "rb 0 2", "rf 1 2", "rb 1 2",
+    "comp 0 1", "oy 1 3", "ox 1 3", "comp 1 1", "rn 1 2", "sec 1 2", "comp 0 3", "rb 0 3",
+    "rf 0 3", "fwd 1 3", "sec 0 2", "rf 0 1", "rn 0 1", "rn 0 3", "rb 0 1", "thi 1 2", "rz 1 2",
+    "rb 1 1", "comp 1 3", "rf 1 3", "sec 0 3", "sec 0 1", "rb 1 3", "rn 1 3", "sumB 0",
+    "rf 1 1", "thi 0 2", "rz 0 2", "thi 0 3", "rz 0 3", "sec 1 3", "rn 1 1", "sec 0 B",
+    "rf 1 0", "rf 0 0", "thi 0 1", "rz 0 1", "sec 1 1", "thi 1 3", "sumB 1", "rz 1 3", "rn 0 0",
+    "thi 0 B", "rn 1 0", "sec 0 0", "thi 1 1", "rz 1 1", "sec 1 0", "sec 1 B", "thi 0 0",
+    "fin 0", "thi 1 0", "thi 1 B", "fin 1", "del 0", "del 1",
 )
 GATHER_X = (
-    {"B": True, 0: False, 1: False, 2: True, 3: False},
-    {"B": True, 0: True, 1: False, 2: False, 3: False},
+    {"B": True, 0: False, 1: True, 2: False, 3: True},
+    {"B": True, 0: True, 1: False, 2: True, 3: False},
 )
 REDUCE_X = (
-    {"B": True, 0: True, 1: True, 2: True, 3: True},
     {"B": False, 0: True, 1: False, 2: False, 3: True},
+    {"B": True, 0: False, 1: False, 2: True, 3: True},
 )
 
 
@@ -236,8 +240,11 @@
         for q in offsets:
             zsend[mb, q] = links.copy(gat_a.at[mb, me], gat_a.at[mb, me], zp[q])
             rz[mb, q] = links.copy(hold2.at[mb, q], rsz.at[mb, q], zp[q])
-            quad = gat_b.at[mb, pl.ds(z * QUAD, QUAD)]
-            bsend[mb, q] = links.copy(quad, quad, zp[q])
+            for up in (1, -1):
+                source = jnp.clip(z - up * (q - 1), 0, depth - 1)
+                quad = gat_b.at[mb, pl.ds(source * QUAD, QUAD)]
+                peer = base + jnp.clip(z + up, 0, depth - 1) * QUAD + lo
+                bsend[mb, q, up] = links.copy(quad, quad, peer)
             theirs = par_b.at[mb, pl.ds(xor(z, q) * QUAD, QUAD)]
             rb[mb, q] = links.copy(theirs, zgot_b.at[mb, q], zp[q])
         for step in ["B"] + list(range(depth)):
@@ -290,11 +297,10 @@
     def do_zs(mb, q):
         links.start(zsend[mb, q])
 
-    def do_own(mb, step):
+    def do_own(mb, step, copies):
         if step != "B" and step > 0:
             await_all(zsend[mb, step])
-        links.start(own_x[mb, step])
-        links.start(own_y[mb, step])
+        links.start(copies[mb, step])
 
     def do_fwd(mb, step):
         await_all((own_y if GATHER_X[mb][step] else own_x)[mb, step])
@@ -303,18 +309,52 @@
     def await_quad(mb, step):
         await_all(own_x[mb, step], own_y[mb, step], forward[mb, step])
 
-    def do_bsend(mb, q):
-        await_quad(mb, "B")
-        links.start(bsend[mb, q])
+    def do_bsend(mb, hop):
+        if hop == 1:
+            await_quad(mb, "B")
+        for up in (1, -1):
+            source, onward = z - up * (hop - 1), z + up
+            held = (source >= 0) & (source < depth)
+            if hop > 1:
+
+                @pl.when(held)
+                def _():
+                    bsend[mb, hop - 1, up].wait_recv()
+
+            @pl.when(held & (onward >= 0) & (onward < depth))
+            def _():
+                bsend[mb, hop, up].start()
+
+    def finish_bsend(mb):
+        for hop in range(1, depth):
+            for up in (1, -1):
+                source, onward = z - up * (hop - 1), z + up
+                held = (source >= 0) & (source < depth)
+
+                @pl.when(held & (onward >= 0) & (onward < depth))
+                def _():
+                    bsend[mb, hop, up].wait_send()
+
+    ended = []
+
+    def last_hop(mb):
+        if mb not in ended:
+            ended.append(mb)
+            for up in (1, -1):
+                source = z - up * (depth - 1)
+
+                @pl.when((source >= 0) & (source < depth))
+                def _():
+                    bsend[mb, depth - 1, up].wait_recv()
 
     ready = []
 
     def do_compute(mb, q):
         await_quad(mb, q)
-        if q > 0:
-            await_all(bsend[mb, q])
-        else:
+        if q == 0:
             await_quad(mb, "B")
+        elif q == depth - 1:
+            last_hop(mb)
         if not ready:
             ready.append(True)
             for copy in load_w:
@@ -368,10 +408,6 @@
             packed = narrow(dot(pack, yb[b]))
             par_a[mb, group + b] = packed[:, :cut]
             par_b[mb, group + b] = packed[:, cut:]
-        if q > 0:
-            links.start(rb[mb, q])
-        for copy in r1[mb, q]:
-            links.start(copy)
         if mb == 1:
             for copy in dots_sent[q]:
                 links.start(copy)
@@ -405,8 +441,6 @@
             sums[mb, :, pl.ds(cut, width - cut)] = total
         else:
             hold2[mb, step] = total
-            if step > 0:
-                links.start(rz[mb, step])
 
     def do_finish(mb):
         total = wide(hold2[mb, 0])
@@ -445,10 +479,15 @@
     events = {
         "place": do_place,
         "zs": do_zs,
-        "own": do_own,
+        "ox": lambda mb, step: do_own(mb, step, own_x),
+        "oy": lambda mb, step: do_own(mb, step, own_y),
         "fwd": do_fwd,
         "zB": do_bsend,
         "comp": do_compute,
+        "rb": lambda mb, q: links.start(rb[mb, q]),
+        "rf": lambda mb, q: links.start(r1[mb, q][0]),
+        "rn": lambda mb, q: links.start(r1[mb, q][1]),
+        "rz": lambda mb, q: links.start(rz[mb, q]),
         "sumB": do_gather_b,
         "sec": do_second,
         "thi": do_third,
@@ -460,6 +499,8 @@
         events[event](*(step if step == "B" else int(step) for step in at))
         if entry == TABLES_AFTER and hop:
             send_tables()
+    for mb in range(2):
+        finish_bsend(mb)
     for copy in links.sent:
         copy.wait_send()
 

time: 90.4 us -> 86.9 us (0.961)
  Pallas kernels: 89.4 us -> 85.9 us
    pallas_call x1, Pallas kernels: 85.4 us -> 81.9 us  [run_layer(): pl.pallas_call(functools.partial(layer_kernel, slices, chunks, rows, hop)...]
where the time goes in v4:
time: 86.9 us; the launch traced here: 86.7 us
  Pallas kernels  85.9 us (99%)
    pallas_call x1, Pallas kernels, run_layer(): pl.pallas_call(functools.partial(layer_kernel, slices, chunks, rows, hop)...  81.9 us
    pallas_call x1, Pallas kernels, mix(): pl.pallas_call(functools.partial(mix_kernel, rows, bool(grading)), out_sh...  3.99 us

profile of v4, /device:TPU:1, one launch (start us, length us, event | category | flops | bytes accessed | tf_op | source)
XLA Modules:
  0.0 86.7 jit_solution(13004808709011131279)
XLA Ops:
  0.6 81.9 %moe_layer.1 = (bf16[80,896]{1,0:T(8,128)(2,1)}, bf16[80,896]{1,0:T(8,128)(2,1)}, f32[16,128]{1,0:T(8,128)}, f32[2,128,128]{2,1,0:T(8,128)}) custom-call(bf16[128,7168]{1,0:T(8,128)(2,1)} %bitcast.24, bf16[128,7168]{1,0:T(8,128)(2,1)} %bitcast.25, bf16[7168,128]{1,0:T(8,128)(2,1)} %bitcast.26, bf16[7168,128]{1,0:T(8,128)(2,1)} %bitcast.27, ...), custom_call_target="tpu_custom_call" | custom-call | tf_op jit(solution)/shard_map/moe_layer/pallas_call | solution.py:531
  82.5 4.0 %mix.1 = (bf16[128,7168]{1,0:T(8,128)(2,1)}, bf16[128,7168]{1,0:T(8,128)(2,1)}, f32[8,128]{1,0:T(8,128)}) custom-call(bf16[80,896]{1,0:T(8,128)(2,1)} %get-tuple-element.10.refs_0_, bf16[80,896]{1,0:T(8,128)(2,1)} %get-tuple-element.11.refs_1_, f32[2,128,128]{2,1,0:T(8,128)} %get-tuple-element.12.refs_2_, f32[16,128]{1,0:T(8,128)} %get-tuple-element.13.refs_3_, ...), custom_call_target="tpu_custom_call" | custom-call | tf_op jit(solution)/shard_map/mix/pallas_call | solution.py:618

commit v5 on v4

--- a/solution.py
+++ b/solution.py
@@ -11,32 +11,33 @@
 FF = 2048
 QUAD = 4
 LANES = 128
-SEMAPHORES = 160
+SEMAPHORES = 192
+SPLIT = (1, 2)
 TABLES_AFTER = "fwd 0 B"
 MESH = pl.DeviceIdType.MESH
 
 SCHEDULE = (
-    "place 0", "oy 0 B", "ox 0 0", "zs 0 2", "zs 0 1", "place 1", "oy 1 0", "zs 1 2", "ox 0 B",
-    "oy 1 B", "ox 1 0", "oy 0 0", "zs 1 1", "fwd 0 0", "ox 1 B", "fwd 0 B", "fwd 1 0",
-    "fwd 1 B", "ox 0 1", "oy 0 2", "oy 0 1", "zs 0 3", "ox 0 2", "zB 0 1", "comp 0 0", "zB 1 1",
-    "ox 1 1", "oy 1 2", "ox 1 2", "comp 1 0", "fwd 0 2", "zB 0 2", "fwd 1 2", "oy 0 3",
-    "fwd 0 1", "zB 1 2", "ox 0 3", "oy 1 1", "zB 0 3", "zs 1 3", "fwd 1 1", "comp 0 2",
-    "rf 0 2", "zB 1 3", "fwd 0 3", "rn 0 2", "comp 1 2", "rb 0 2", "rf 1 2", "rb 1 2",
-    "comp 0 1", "oy 1 3", "ox 1 3", "comp 1 1", "rn 1 2", "sec 1 2", "comp 0 3", "rb 0 3",
-    "rf 0 3", "fwd 1 3", "sec 0 2", "rf 0 1", "rn 0 1", "rn 0 3", "rb 0 1", "thi 1 2", "rz 1 2",
-    "rb 1 1", "comp 1 3", "rf 1 3", "sec 0 3", "sec 0 1", "rb 1 3", "rn 1 3", "sumB 0",
-    "rf 1 1", "thi 0 2", "rz 0 2", "thi 0 3", "rz 0 3", "sec 1 3", "rn 1 1", "sec 0 B",
-    "rf 1 0", "rf 0 0", "thi 0 1", "rz 0 1", "sec 1 1", "thi 1 3", "sumB 1", "rz 1 3", "rn 0 0",
-    "thi 0 B", "rn 1 0", "sec 0 0", "thi 1 1", "rz 1 1", "sec 1 0", "sec 1 B", "thi 0 0",
-    "fin 0", "thi 1 0", "thi 1 B", "fin 1", "del 0", "del 1",
+    "place 0", "ox 0 0", "oy 0 0", "zs 0 1", "place 1", "oy 1 B", "oy 0 B", "ox 1 0", "zs 1 1",
+    "oy 1 0", "ox 1 B", "ox 0 B", "zs 0 2", "ox 0 1", "oy 0 1", "fwd 1 B", "fwd 0 0", "zs 1 2",
+    "oy 1 1", "fwd 0 B", "zs 0 3", "ox 1 1", "oy 0 2", "zs 1 3", "ox 1 2", "zB 1 1", "oy 1 2",
+    "zB 0 1", "oy 0 3", "ox 0 3", "ox 1 3", "fwd 1 1", "comp 0 0", "ox 0 2", "fwd 1 2",
+    "oy 1 3", "fwd 0 2", "zB 1 2", "fwd 0 1", "zB 0 2", "fwd 0 3", "comp 1 1", "zB 1 3",
+    "fwd 1 3", "rf 1 1", "comp 1 2", "rb 1 2", "zB 0 3", "rf 1 2", "rn 1 1", "comp 0 2",
+    "rn 1 2", "rb 0 2", "rb 1 1", "fwd 1 0", "rf 0 2", "rn 0 2", "comp 1 3", "sec 1 2",
+    "rb 1 3", "sec 1 1", "comp 0 3", "rf 0 3", "rb 0 3", "comp 0 1", "rf 0 1", "sec 0 2",
+    "rf 1 3", "rb 0 1", "rn 0 3", "thi 1 2", "rz 1 2", "sec 0 3", "thi 0 2", "sumB 0", "rn 0 1",
+    "thi 1 1", "rz 0 2", "rz 1 1", "rn 1 3", "sec 0 1", "comp 1 0", "sec 1 3", "sumB 1",
+    "thi 0 3", "rf 0 0", "rz 0 3", "rn 0 0", "rf 1 0", "sec 0 B", "thi 1 3", "rz 1 3",
+    "thi 0 1", "rn 1 0", "sec 1 B", "rz 0 1", "sec 0 0", "sec 1 0", "thi 1 B", "thi 0 B",
+    "thi 0 0", "fin 0", "thi 1 0", "fin 1", "del 0", "del 1",
 )
 GATHER_X = (
-    {"B": True, 0: False, 1: True, 2: False, 3: True},
-    {"B": True, 0: True, 1: False, 2: True, 3: False},
+    {"B": False, 0: True, 1: True, 2: True, 3: False},
+    {"B": True, 0: True, 1: False, 2: False, 3: False},
 )
 REDUCE_X = (
     {"B": False, 0: True, 1: False, 2: False, 3: True},
-    {"B": True, 0: False, 1: False, 2: True, 3: True},
+    {"B": False, 0: False, 1: True, 2: False, 3: True},
 )
 
 
@@ -140,8 +141,8 @@
     outs = 4 if hop else 3
     out_f, out_b, out_dots = refs[inputs : inputs + 3]
     (
-        tok, wc, wd, gat_a, gat_b, par_a, par_b, xb, yb, pre, rs1, rs2, rsz, hold, hold2, zgot_b,
-        sum_b, rs1_b, rs2_b, hold_b, sums, landed, table, table_got, dot_out, dot_in, local_sems,
+        tok, wc, wd, gat_a0, gat_b0, gat_a1, gat_b1, par_a, par_b, xb, yb, pre, rs1, rs2, rsz, hold, hold2, zgot_b,
+        sum_b, rs1_b, rs2_b, hold_b, sums, landed, table, table_got, dot_out, dot_in, ids_got, gates_got, pre_got, local_sems,
         send_sems, recv_sems,
     ) = refs[inputs + outs :]
     device = lax.axis_index("expert")
@@ -156,7 +157,8 @@
     features, ff = wc.shape[0], wd.shape[0]
     width = features // chunks
     pad = padded(rows)
-    cut = gat_a.shape[3]
+    gat_a, gat_b = (gat_a0, gat_a1), (gat_b0, gat_b1)
+    cut = par_a.shape[3]
 
     def bid(q, mask):
         return xor(z, q) * QUAD + xor(lo, mask)
@@ -172,6 +174,9 @@
         copy.start()
         return copy
 
+    load_route = []
+    for k in range(len(routes)):
+        load_route.append(load(routes[k], (gates_got if k % 2 else ids_got).at[k // 2]))
     load_f = [load(tok_f.at[:, cols_of(j)], tok.at[0, :, cols_of(j)]) for j in range(chunks)]
 
     barrier = pltpu.get_barrier_semaphore()
@@ -199,6 +204,8 @@
             load_w.append(load(w_gate.at[cols_of(j), :], wc.at[cols_of(j), pl.ds(0, ff)]))
             load_w.append(load(w_up.at[cols_of(j), :], wc.at[cols_of(j), pl.ds(ff, ff)]))
             load_w.append(load(w_down.at[:, cols_of(j)], wd.at[:, cols_of(j)]))
+        load_w.append(load(pre_gate, pre_got.at[0]))
+        load_w.append(load(pre_up, pre_got.at[1]))
 
     unpack = selection(chunks, rows, pad)
     pack = selection(chunks, rows, pad, flip=True)
@@ -210,13 +217,14 @@
             return narrow(
                 jnp.where(same == lax.broadcasted_iota(jnp.int32, shape, 1), 1.0, 0.0)
             )
-        ids = routes[2 * mb][...]
-        return narrow(slot_rows(ids, pad))
+        load_route[2 * mb].wait()
+        return narrow(slot_rows(ids_got[mb], pad))
 
     def send_tables():
         for mb in range(2):
-            ids = routes[2 * mb][...]
-            gates = jnp.where(ids == 0, routes[2 * mb + 1][...], 0.0)
+            load_route[2 * mb + 1].wait()
+            ids = ids_got[mb]
+            gates = jnp.where(ids == 0, gates_got[mb], 0.0)
             weighted = slot_rows(ids, LANES) * jnp.sum(gates, axis=0, keepdims=True)
             table[mb] = jnp.transpose(weighted)
             links.start(tables[mb])
@@ -229,8 +237,9 @@
             picked = dot(chosen, tok[mb, :, cols_of(j)])
             yb[0, pl.ds(j * pad, pad), :] = narrow(picked)
         packed = narrow(dot(pack, yb[0]))
-        gat_a[mb, me] = packed[:, :cut]
-        gat_b[mb, me] = packed[:, cut:]
+        edge = gat_a[mb].shape[2]
+        gat_a[mb][me] = packed[:, :edge]
+        gat_b[mb][me] = packed[:, edge:]
 
     links = Links(send_sems, recv_sems)
     offsets = range(1, depth)
@@ -238,23 +247,24 @@
     zsend, rz, bsend, rb, dots_sent = {}, {}, {}, {}, {}
     for mb in range(2):
         for q in offsets:
-            zsend[mb, q] = links.copy(gat_a.at[mb, me], gat_a.at[mb, me], zp[q])
             rz[mb, q] = links.copy(hold2.at[mb, q], rsz.at[mb, q], zp[q])
             for up in (1, -1):
                 source = jnp.clip(z - up * (q - 1), 0, depth - 1)
-                quad = gat_b.at[mb, pl.ds(source * QUAD, QUAD)]
                 peer = base + jnp.clip(z + up, 0, depth - 1) * QUAD + lo
+                block = gat_a[mb].at[source * QUAD + lo]
+                zsend[mb, q, up] = links.copy(block, block, peer)
+                quad = gat_b[mb].at[pl.ds(source * QUAD, QUAD)]
                 bsend[mb, q, up] = links.copy(quad, quad, peer)
             theirs = par_b.at[mb, pl.ds(xor(z, q) * QUAD, QUAD)]
             rb[mb, q] = links.copy(theirs, zgot_b.at[mb, q], zp[q])
         for step in ["B"] + list(range(depth)):
             at = (mb, step)
-            q, gat = (0, gat_b) if step == "B" else (step, gat_a)
-            block = gat.at[mb, bid(q, 0)]
+            q, gat = (0, gat_b[mb]) if step == "B" else (step, gat_a[mb])
+            block = gat.at[bid(q, 0)]
             own_x[at] = links.copy(block, block, xp)
             own_y[at] = links.copy(block, block, yp)
             via_x = GATHER_X[mb][step]
-            got = gat.at[mb, bid(q, 2 if via_x else 1)]
+            got = gat.at[bid(q, 2 if via_x else 1)]
             forward[at] = links.copy(got, got, xp if via_x else yp)
             m1, p1, p2 = (1, xp, yp) if REDUCE_X[mb][step] else (2, yp, xp)
             if step == "B":
@@ -294,24 +304,7 @@
         if mb == 0:
             pl.semaphore_wait(barrier, greeted)
 
-    def do_zs(mb, q):
-        links.start(zsend[mb, q])
-
-    def do_own(mb, step, copies):
-        if step != "B" and step > 0:
-            await_all(zsend[mb, step])
-        links.start(copies[mb, step])
-
-    def do_fwd(mb, step):
-        await_all((own_y if GATHER_X[mb][step] else own_x)[mb, step])
-        links.start(forward[mb, step])
-
-    def await_quad(mb, step):
-        await_all(own_x[mb, step], own_y[mb, step], forward[mb, step])
-
-    def do_bsend(mb, hop):
-        if hop == 1:
-            await_quad(mb, "B")
+    def chain(sends, mb, hop):
         for up in (1, -1):
             source, onward = z - up * (hop - 1), z + up
             held = (source >= 0) & (source < depth)
@@ -319,13 +312,25 @@
 
                 @pl.when(held)
                 def _():
-                    bsend[mb, hop - 1, up].wait_recv()
+                    sends[mb, hop - 1, up].wait_recv()
 
             @pl.when(held & (onward >= 0) & (onward < depth))
             def _():
-                bsend[mb, hop, up].start()
-
-    def finish_bsend(mb):
+                sends[mb, hop, up].start()
+
+    ended = []
+
+    def last_hop(sends, mb):
+        if (sends is bsend, mb) not in ended:
+            ended.append((sends is bsend, mb))
+            for up in (1, -1):
+                source = z - up * (depth - 1)
+
+                @pl.when((source >= 0) & (source < depth))
+                def _():
+                    sends[mb, depth - 1, up].wait_recv()
+
+    def finish_chain(sends, mb):
         for hop in range(1, depth):
             for up in (1, -1):
                 source, onward = z - up * (hop - 1), z + up
@@ -333,19 +338,27 @@
 
                 @pl.when(held & (onward >= 0) & (onward < depth))
                 def _():
-                    bsend[mb, hop, up].wait_send()
-
-    ended = []
-
-    def last_hop(mb):
-        if mb not in ended:
-            ended.append(mb)
-            for up in (1, -1):
-                source = z - up * (depth - 1)
-
-                @pl.when((source >= 0) & (source < depth))
-                def _():
-                    bsend[mb, depth - 1, up].wait_recv()
+                    sends[mb, hop, up].wait_send()
+
+    def do_zs(mb, hop):
+        chain(zsend, mb, hop)
+
+    def do_own(mb, step, copies):
+        if step == depth - 1:
+            last_hop(zsend, mb)
+        links.start(copies[mb, step])
+
+    def do_fwd(mb, step):
+        await_all((own_y if GATHER_X[mb][step] else own_x)[mb, step])
+        links.start(forward[mb, step])
+
+    def await_quad(mb, step):
+        await_all(own_x[mb, step], own_y[mb, step], forward[mb, step])
+
+    def do_bsend(mb, hop):
+        if hop == 1:
+            await_quad(mb, "B")
+        chain(bsend, mb, hop)
 
     ready = []
 
@@ -354,23 +367,25 @@
         if q == 0:
             await_quad(mb, "B")
         elif q == depth - 1:
-            last_hop(mb)
+            last_hop(bsend, mb)
         if not ready:
             ready.append(True)
             for copy in load_w:
                 copy.wait()
             spaced = selection(slices, rows, pad)
-            for k, saved in enumerate((pre_gate, pre_up)):
-                pre[k] = narrow(dot(spaced, saved[...])).reshape(pre.shape[1:])
+            for k in range(2):
+                pre[k] = narrow(dot(spaced, pre_got[k])).reshape(pre.shape[1:])
         zq = xor(z, q)
         group = zq * QUAD
         for b in range(QUAD):
-            full_a = narrow(dot(unpack, gat_a[mb, group + b]))
-            full_b = narrow(dot(unpack, gat_b[mb, group + b]))
+            full_a = narrow(dot(unpack, gat_a[mb][group + b]))
+            full_b = narrow(dot(unpack, gat_b[mb][group + b]))
+            edge = full_a.shape[1]
             for j in range(chunks):
                 piece_rows = slice(j * pad, (j + 1) * pad)
-                xb[pl.ds(b * pad, pad), pl.ds(j * width, cut)] = full_a[piece_rows]
-                xb[pl.ds(b * pad, pad), pl.ds(j * width + cut, width - cut)] = full_b[piece_rows]
+                xb[pl.ds(b * pad, pad), pl.ds(j * width, edge)] = full_a[piece_rows]
+                after = pl.ds(j * width + edge, width - edge)
+                xb[pl.ds(b * pad, pad), after] = full_b[piece_rows]
         total = None
         for j in range(chunks):
             if mb == 0:
@@ -500,7 +515,8 @@
         if entry == TABLES_AFTER and hop:
             send_tables()
     for mb in range(2):
-        finish_bsend(mb)
+        finish_chain(zsend, mb)
+        finish_chain(bsend, mb)
     for copy in links.sent:
         copy.wait_send()
 
@@ -516,11 +532,16 @@
     group = QUAD * pad
 
     vmem = pl.BlockSpec(memory_space=pltpu.VMEM)
-    anywhere = pl.BlockSpec(memory_space=pl.ANY)
+    anywhere = pl.BlockSpec(memory_space=pltpu.HBM)
     block = (chunks * rows, width)
     last = max(width // LANES // 7, 1) * LANES
+    gathers = []
+    for sevenths in SPLIT:
+        for columns in (width - sevenths * last, sevenths * last):
+            gathers.append(pltpu.VMEM((slices, chunks * rows, columns), jnp.bfloat16))
     part_a, part_b = (chunks * rows, width - last), (chunks * rows, last)
     tables = (2, tok_f.shape[0] if hop else 8, LANES)
+    choices = routes[0].shape if hop else (8, LANES)
     out_shape = [
         jax.ShapeDtypeStruct(block, jnp.bfloat16),
         jax.ShapeDtypeStruct(block, jnp.bfloat16),
@@ -531,14 +552,13 @@
     return pl.pallas_call(
         functools.partial(layer_kernel, slices, chunks, rows, hop),
         out_shape=tuple(out_shape),
-        in_specs=[anywhere] * 5 + [vmem] * (2 + len(routes)),
+        in_specs=[anywhere] * (7 + len(routes)),
         out_specs=(vmem,) * len(out_shape),
         scratch_shapes=[
             pltpu.VMEM((2,) + tok_f.shape, jnp.bfloat16),
             pltpu.VMEM((features, 2 * ff), jnp.bfloat16),
             pltpu.VMEM((ff, features), jnp.bfloat16),
-            pltpu.VMEM((2, slices) + part_a, jnp.bfloat16),
-            pltpu.VMEM((2, slices) + part_b, jnp.bfloat16),
+            *gathers,
             pltpu.VMEM((2, slices) + part_a, jnp.bfloat16),
             pltpu.VMEM((2, slices) + part_b, jnp.bfloat16),
             pltpu.VMEM((group, features), jnp.bfloat16),
@@ -560,7 +580,10 @@
             pltpu.VMEM(tables, jnp.float32),
             pltpu.VMEM((slices, pad, LANES), jnp.float32),
             pltpu.VMEM((slices, pad, LANES), jnp.float32),
-            pltpu.SemaphoreType.DMA((5 * chunks,)),
+            pltpu.VMEM((2,) + choices, jnp.int32),
+            pltpu.VMEM((2,) + choices, jnp.float32),
+            pltpu.VMEM((2,) + pre_gate.shape, jnp.bfloat16),
+            pltpu.SemaphoreType.DMA((5 * chunks + 6,)),
             pltpu.SemaphoreType.DMA((SEMAPHORES,)),
             pltpu.SemaphoreType.DMA((SEMAPHORES,)),
         ],
@@ -624,6 +647,7 @@
             pltpu.VMEM((2, tokens, chunks * width), jnp.bfloat16),
             pltpu.SemaphoreType.DMA((2 * chunks,)),
         ],
+
         name="mix",
     )(block_f, block_b, tables, *grading)
 

time: 86.9 us -> 84.4 us (0.971)
  Pallas kernels: 85.9 us -> 83.4 us
    pallas_call x1, Pallas kernels: 81.9 us -> 79.4 us  [run_layer(): pl.pallas_call(functools.partial(layer_kernel, slices, chunks, rows, hop)...]
where the time goes in v5:
time: 84.4 us; the launch traced here: 84.2 us
  Pallas kernels  83.4 us (99%)
    pallas_call x1, Pallas kernels, run_layer(): pl.pallas_call(functools.partial(layer_kernel, slices, chunks, rows, hop)...  79.4 us
    pallas_call x1, Pallas kernels, mix(): pl.pallas_call(functools.partial(mix_kernel, rows, bool(grading)), out_sh...  3.99 us

profile of v5, /device:TPU:1, one launch (start us, length us, event | category | flops | bytes accessed | tf_op | source)
XLA Modules:
  0.0 84.2 jit_solution(13853551132281983398)
XLA Ops:
  0.6 79.4 %moe_layer.1 = (bf16[80,896]{1,0:T(8,128)(2,1)}, bf16[80,896]{1,0:T(8,128)(2,1)}, f32[16,128]{1,0:T(8,128)}, f32[2,128,128]{2,1,0:T(8,128)}) custom-call(bf16[128,7168]{1,0:T(8,128)(2,1)} %bitcast.24, bf16[128,7168]{1,0:T(8,128)(2,1)} %bitcast.25, bf16[7168,128]{1,0:T(8,128)(2,1)} %bitcast.26, bf16[7168,128]{1,0:T(8,128)(2,1)} %bitcast.27, ...), custom_call_target="tpu_custom_call" | custom-call | tf_op jit(solution)/shard_map/moe_layer/pallas_call | solution.py:552
  80.1 4.0 %mix.1 = (bf16[128,7168]{1,0:T(8,128)(2,1)}, bf16[128,7168]{1,0:T(8,128)(2,1)}, f32[8,128]{1,0:T(8,128)}) custom-call(bf16[80,896]{1,0:T(8,128)(2,1)} %get-tuple-element.10.refs_0_, bf16[80,896]{1,0:T(8,128)(2,1)} %get-tuple-element.11.refs_1_, f32[2,128,128]{2,1,0:T(8,128)} %get-tuple-element.12.refs_2_, f32[16,128]{1,0:T(8,128)} %get-tuple-element.13.refs_3_, ...), custom_call_target="tpu_custom_call" | custom-call | tf_op jit(solution)/shard_map/mix/pallas_call | solution.py:641
